TPU v7x, 256 devices: a whole 4x4x8 slice. The times are simulated.
256 devices in a mesh: gx: 8 (over z_lo, core), gy: 4 (over y), gz: 8 (over z_hi, x).
Axes of the slice: x: 4, y: 4, z: 8 (z_hi: 2, z_lo: 4; z = z_hi * 4 + z_lo), core: 2. Of those that a mesh axis runs over, the one named last changes fastest.
Arguments:
- raw_weight: float32 [128, 27, 128], P(('gx', 'gy')), may hold values from -6 to 6
- inputs: bfloat16 [64, 64, 128, 128], P('gx', 'gy', 'gz'), may hold values from -6 to 6
- cotangent: bfloat16 [64, 64, 128, 128], P('gx', 'gy', 'gz'), may hold values from -0.099609375 to 0.099609375
Outputs:
- input_grad: bfloat16 [64, 64, 128, 128], P('gx', 'gy', 'gz')
- weight_grad: float32 [128, 27, 128], P(('gx', 'gy'))
All inputs are finite; a program needn't handle non-finite values.
Results may differ from a plain program's by a relative error of at most 0.0049.
Values may be sent and summed in bfloat16 or wider, within the bound.
A program may use at most 64 MiB of HBM per device.

v0:
```python
import functools

import jax
import jax.numpy as jnp
from jax import lax
from jax.experimental import pallas as pl
from jax.experimental.pallas import tpu as pltpu
from jax.sharding import PartitionSpec as P

var_eps = 1e-05
norm_eps = 1e-06
clip_norm = 600.0
F32 = jnp.float32
BF16 = jnp.bfloat16
MESH = pl.DeviceIdType.MESH
AXES = ("gx", "gy", "gz")


def kernel(dims, raw_hbm, in_hbm, cot_hbm, dx_ref, wg_ref, *scratch):
    (raw_ref, in_ref, shifted, face_out, face_in, in_t, part, recv_x, send_y, recv_y, send_z, recv_z, full, std,
     std_all, w_cat, stats, stats_in, load_sem, halo_send, halo_recv, x_send, x_recv, y_send, y_recv,
     z_send, z_recv, g_send, g_recv, ay_send, ay_recv, ax_send, ax_recv, st_send, st_recv) = scratch
    count = dict(zip(AXES, dims))
    nx, ny, nz = dims
    plane_peers = nx * ny - 1
    me = {axis: lax.axis_index(axis) for axis in AXES}
    taps, rows, chan = raw_ref.shape
    ex, ey, ez = in_ref.shape[:3]
    padded_taps = send_z.shape[0]
    piece = padded_taps // nz
    fan_count = float(rows * nx * ny * taps)

    def peer(axis, k):
        return lax.rem(me[axis] + k, count[axis])

    def plane_peer(k):
        flat = lax.rem(me["gx"] * ny + me["gy"] + k, nx * ny)
        return {"gx": lax.div(flat, ny), "gy": lax.rem(flat, ny)}

    def remote(src, dst, send_sem, recv_sem, where):
        return pltpu.make_async_remote_copy(
            src_ref=src, dst_ref=dst, send_sem=send_sem, recv_sem=recv_sem,
            device_id=where, device_id_type=MESH,
        )

    def wait_all(copies):
        for copy in copies:
            copy.wait()

    body = pl.ds(1, ey)
    load_raw = pltpu.make_async_copy(raw_hbm, raw_ref, load_sem.at[0])
    load_cot = pltpu.make_async_copy(cot_hbm, shifted.at[1, pl.ds(1, ex), body], load_sem.at[1])
    load_in = pltpu.make_async_copy(in_hbm, in_ref, load_sem.at[2])
    load_raw.start()
    load_cot.start()
    load_in.start()

    barrier = pltpu.get_barrier_semaphore()
    for k in range(1, nx * ny):
        pl.semaphore_signal(barrier, inc=1, device_id=plane_peer(k), device_id_type=MESH)
    for k in range(1, nz):
        pl.semaphore_signal(barrier, inc=1, device_id={"gz": peer("gz", k)}, device_id_type=MESH)

    def exchange_start(slot, base, peers):
        copies = []
        for k, where in enumerate(peers):
            copy = remote(stats.at[slot], stats_in.at[base + k], st_send.at[base + k], st_recv.at[base + k], where)
            copy.start()
            copies.append(copy)
        return copies

    def exchange_sum(slot, base, copies):
        wait_all(copies)
        total = stats[slot]
        for k in range(len(copies)):
            total = total + stats_in[base + k]
        return total

    zero_plane = jnp.zeros((ey, ez, chan), BF16)
    zero_col = jnp.zeros((ex + 2, ez, chan), BF16)
    zero_face = jnp.zeros((ex + 2, ey + 2, chan), BF16)

    @pl.when(me["gx"] == 0)
    def _():
        shifted[1, 0, 1:ey + 1] = zero_plane

    @pl.when(me["gx"] == nx - 1)
    def _():
        shifted[1, ex + 1, 1:ey + 1] = zero_plane

    @pl.when(me["gy"] == 0)
    def _():
        shifted[1, :, 0] = zero_col

    @pl.when(me["gy"] == ny - 1)
    def _():
        shifted[1, :, ey + 1] = zero_col

    @pl.when(me["gz"] == 0)
    def _():
        face_in[0] = zero_face

    @pl.when(me["gz"] == nz - 1)
    def _():
        face_in[1] = zero_face

    for t in range(taps, padded_taps):
        send_z[t] = jnp.zeros((rows, chan), BF16)
        std[t] = jnp.zeros((rows, chan), F32)

    load_raw.wait()

    def per_output(value):
        return jnp.sum(jnp.sum(value, axis=0), axis=0, keepdims=True)

    raw = raw_ref[...]
    stats[0] = jnp.concatenate([per_output(raw), per_output(raw * raw), jnp.zeros((6, chan), F32)], axis=0)
    load_cot.wait()
    pl.semaphore_wait(barrier, plane_peers + nz - 1)

    def halo(axis, number, low_src, high_dst, high_src, low_dst):
        lower, upper = lax.max(me[axis] - 1, 0), lax.min(me[axis] + 1, count[axis] - 1)
        down = remote(low_src, high_dst, halo_send.at[2 * number], halo_recv.at[2 * number], {axis: lower})
        up = remote(high_src, low_dst, halo_send.at[2 * number + 1], halo_recv.at[2 * number + 1], {axis: upper})

        @pl.when(me[axis] > 0)
        def _():
            down.start()

        @pl.when(me[axis] < count[axis] - 1)
        def _():
            up.start()

        def finish():
            @pl.when(me[axis] > 0)
            def _():
                down.wait_send()
                up.wait_recv()

            @pl.when(me[axis] < count[axis] - 1)
            def _():
                up.wait_send()
                down.wait_recv()

        return finish

    halo_x = halo("gx", 0, shifted.at[1, 1, body], shifted.at[1, ex + 1, body],
                  shifted.at[1, ex, body], shifted.at[1, 0, body])
    weight_sums = exchange_start(0, 0, [plane_peer(k) for k in range(1, nx * ny)])
    load_in.wait()
    for x in range(ex):
        in_t[:, x * ey * ez:(x + 1) * ey * ez] = in_ref[x].reshape(ey * ez, chan).T
    halo_x()
    halo_y = halo("gy", 1, shifted.at[1, :, 1], shifted.at[1, :, ey + 1],
                  shifted.at[1, :, ey], shifted.at[1, :, 0])

    sums = exchange_sum(0, 0, weight_sums)
    mean_out = sums[0:1] / fan_count
    var_out = sums[1:2] / fan_count - mean_out * mean_out
    inv_std = lax.rsqrt(var_out + var_eps)
    order = [t for c in (1, 0, 2) for t in range(c, taps, 3)]
    own = std_all.at[me["gx"], me["gy"]]
    for u, t in enumerate(order):
        value = (raw_ref[t] - mean_out) * inv_std
        std[u] = value
        own[u] = value.astype(BF16)
    gather_y = []
    for k in range(1, ny):
        copy = remote(own, own, ay_send.at[k - 1], ay_recv.at[k - 1], {"gy": peer("gy", k)})
        copy.start()
        gather_y.append(copy)

    halo_y()
    for x in range(ex + 2):
        plane = shifted[1, x].astype(F32)
        face_out[0, x] = plane[:, 0, :].astype(BF16)
        face_out[1, x] = plane[:, ez - 1, :].astype(BF16)
    halo_z = halo("gz", 2, face_out.at[0], face_in.at[1], face_out.at[1], face_in.at[0])

    def view(t, start, planes):
        a, b, c = t // 9, (t // 3) % 3, t % 3
        block = shifted[2 - c, pl.ds(start + 2 - a, planes), 2 - b:2 - b + ey]
        return block.reshape(planes * ey * ez, chan)

    chunk = taps // 3

    def filter_chunk(n):
        for u in range(n * chunk, (n + 1) * chunk, 2):
            group = list(range(u, min(u + 2, (n + 1) * chunk)))
            views = [view(order[v], 0, ex) for v in group]
            right = jnp.concatenate(views, axis=1) if len(views) > 1 else views[0]
            product = jnp.dot(in_t[...], right, preferred_element_type=F32)
            for j, v in enumerate(group):
                for gx in range(nx):
                    for gy in range(ny):
                        low = (gx * ny + gy) * rows
                        part[gx, gy, v] = product[low:low + rows, j * chan:(j + 1) * chan]
        copies = []
        span = pl.ds(n * chunk, chunk)
        for k in range(1, nx):
            index = n * (nx - 1) + k - 1
            copy = remote(part.at[peer("gx", k), :, span], recv_x.at[k - 1, :, span],
                          x_send.at[index], x_recv.at[index], {"gx": peer("gx", k)})
            copy.start()
            copies.append(copy)
        return copies

    def rows_chunk(n, copies):
        wait_all(copies)
        span = pl.ds(n * chunk, chunk)
        for gy in range(ny):
            total = part[me["gx"], gy, span]
            for k in range(1, nx):
                total = total + recv_x[k - 1, gy, span]
            send_y[gy, span] = total.astype(BF16)
        sent = []
        for k in range(1, ny):
            index = n * (ny - 1) + k - 1
            copy = remote(send_y.at[peer("gy", k), span], recv_y.at[k - 1, span],
                          y_send.at[index], y_recv.at[index], {"gy": peer("gy", k)})
            copy.start()
            sent.append(copy)
        return sent

    depth_index = lax.broadcasted_iota(jnp.int32, (ey + 2, ez, chan), 1)

    def shift(slot, side, amount, edge):
        for x in range(ex + 2):
            plane = shifted[1, x].astype(F32)
            outer = face_in[side, x].astype(F32)[:, None, :]
            shifted[slot, x] = jnp.where(depth_index == edge, outer, pltpu.roll(plane, amount, 1)).astype(BF16)

    copies_0 = filter_chunk(0)
    halo_z()
    shift(2, 1, ez - 1, ez - 1)
    copies_1 = filter_chunk(1)
    reduce_y = rows_chunk(0, copies_0)
    shift(0, 0, 1, 0)
    copies_2 = filter_chunk(2)
    reduce_y += rows_chunk(1, copies_1)
    wait_all(gather_y)
    gather_x = []
    for k in range(1, nx):
        copy = remote(std_all.at[me["gx"]], std_all.at[me["gx"]], ax_send.at[k - 1], ax_recv.at[k - 1],
                      {"gx": peer("gx", k)})
        copy.start()
        gather_x.append(copy)
    reduce_y += rows_chunk(2, copies_2)

    wait_all(gather_x)
    for u in range(taps):
        w_cat[:, u * chan:(u + 1) * chan] = std_all[:, :, u].reshape(nx * ny * rows, chan)
    step = 2 if ex % 2 == 0 else 1

    def dx_step(n, carry):
        start = n * step
        left = jnp.concatenate([view(t, start, step) for t in order], axis=1)
        product = lax.dot_general(left, w_cat[...], (((1,), (1,)), ((), ())), preferred_element_type=F32)
        dx_ref[pl.ds(start, step)] = product.astype(BF16).reshape(step, ey, ez, chan)
        return carry

    half = ex // step // 2
    lax.fori_loop(0, half, dx_step, 0)

    wait_all(reduce_y)
    total = send_y[me["gy"]].astype(F32)
    for k in range(1, ny):
        total = total + recv_y[k - 1].astype(F32)
    send_z[0:taps] = total.astype(BF16)
    reduce_z = []
    for k in range(1, nz):
        copy = remote(send_z.at[pl.ds(peer("gz", k) * piece, piece)], recv_z.at[k - 1],
                      z_send.at[k - 1], z_recv.at[k - 1], {"gz": peer("gz", k)})
        copy.start()
        reduce_z.append(copy)

    lax.fori_loop(half, ex // step, dx_step, 0)

    wait_all(reduce_z)
    mine = pl.ds(me["gz"] * piece, piece)
    grad = send_z[mine].astype(F32)
    for k in range(1, nz):
        grad = grad + recv_z[k - 1].astype(F32)
    full[mine] = grad
    stats[1] = jnp.concatenate(
        [per_output(grad), per_output(grad * std[mine]), per_output(grad * grad), jnp.zeros((5, chan), F32)], axis=0
    )
    depth_peers = [{"gz": peer("gz", k)} for k in range(1, nz)]
    sums_z = exchange_start(1, plane_peers, depth_peers)
    gather_z = []
    for k in range(1, nz):
        copy = remote(full.at[mine], full.at[mine], g_send.at[k - 1], g_recv.at[k - 1], {"gz": peer("gz", k)})
        copy.start()
        gather_z.append(copy)
    stats[2] = exchange_sum(1, plane_peers, sums_z)
    sums_xy = exchange_start(2, plane_peers + nz - 1, [plane_peer(k) for k in range(1, nx * ny)])
    wait_all(gather_z)
    sums = exchange_sum(2, plane_peers + nz - 1, sums_xy)
    sum_grad, sum_cross, sum_square = sums[0:1], sums[1:2], sums[2:3]
    mean_grad = sum_grad / fan_count
    mean_cross = sum_cross / fan_count
    spread = sum_square - 2.0 * mean_grad * sum_grad - 2.0 * mean_cross * sum_cross
    spread = (
        spread
        + fan_count * mean_grad * mean_grad
        + fan_count * mean_cross * mean_cross * var_out / (var_out + var_eps)
    )
    square_sum = jnp.sum(inv_std * inv_std * spread, axis=1, keepdims=True)
    scale = jnp.minimum(1.0, clip_norm * lax.rsqrt(square_sum + norm_eps))
    factor = inv_std * scale
    for u, t in enumerate(order):
        wg_ref[t] = factor * (full[u] - mean_grad - std[u] * mean_cross)


def on_device(dims, raw_weight, inputs, cotangent):
    nx, ny, nz = dims
    rows, taps, chan = raw_weight.shape
    ex, ey, ez = inputs.shape[:3]
    padded_taps = -(-taps // nz) * nz
    piece = padded_taps // nz
    stat_slots = 2 * (nx * ny - 1) + nz - 1
    dma = pltpu.SemaphoreType.DMA

    def pair(n):
        return [dma((max(n, 1),)), dma((max(n, 1),))]

    scratch = [
        pltpu.VMEM((taps, rows, chan), F32),
        pltpu.VMEM(inputs.shape, BF16),
        pltpu.VMEM((3, ex + 2, ey + 2, ez, chan), BF16),
        pltpu.VMEM((2, ex + 2, ey + 2, chan), BF16),
        pltpu.VMEM((2, ex + 2, ey + 2, chan), BF16),
        pltpu.VMEM((chan, ex * ey * ez), BF16),
        pltpu.VMEM((nx, ny, taps, rows, chan), F32),
        pltpu.VMEM((nx - 1, ny, taps, rows, chan), F32),
        pltpu.VMEM((ny, taps, rows, chan), BF16),
        pltpu.VMEM((ny - 1, taps, rows, chan), BF16),
        pltpu.VMEM((padded_taps, rows, chan), BF16),
        pltpu.VMEM((nz - 1, piece, rows, chan), BF16),
        pltpu.VMEM((padded_taps, rows, chan), F32),
        pltpu.VMEM((padded_taps, rows, chan), F32),
        pltpu.VMEM((nx, ny, taps, rows, chan), BF16),
        pltpu.VMEM((chan, taps * chan), BF16),
        pltpu.VMEM((3, 8, chan), F32),
        pltpu.VMEM((stat_slots, 8, chan), F32),
        dma((3,)), *pair(6), *pair(3 * (nx - 1)), *pair(3 * (ny - 1)), *pair(nz - 1), *pair(nz - 1),
        *pair(ny - 1), *pair(nx - 1), *pair(stat_slots),
    ]
    vmem = pl.BlockSpec(memory_space=pltpu.VMEM)
    anywhere = pl.BlockSpec(memory_space=pl.ANY)
    input_grad, weight_grad = pl.pallas_call(
        functools.partial(kernel, dims),
        out_shape=(
            jax.ShapeDtypeStruct(cotangent.shape, BF16),
            jax.ShapeDtypeStruct((taps, rows, chan), F32),
        ),
        in_specs=[anywhere] * 3,
        out_specs=(vmem, vmem),
        scratch_shapes=scratch,
        compiler_params=pltpu.CompilerParams(
            collective_id=0, has_side_effects=True, vmem_limit_bytes=60 * 1024 * 1024
        ),
    )(jnp.transpose(raw_weight, (1, 0, 2)), inputs, cotangent)
    return input_grad, jnp.transpose(weight_grad, (1, 0, 2))


def solution(mesh):
    dims = tuple(mesh.shape[axis] for axis in AXES)
    in_specs = (P(("gx", "gy"), None, None), P("gx", "gy", "gz", None), P("gx", "gy", "gz", None))
    out_specs = (P("gx", "gy", "gz", None), P(("gx", "gy"), None, None))
    return jax.shard_map(
        functools.partial(on_device, dims), mesh=mesh, in_specs=in_specs, out_specs=out_specs, check_vma=False
    )
```

profile of v0, /device:TPU:1, one launch (start us, length us, event | category | flops | bytes accessed | tf_op | source)
XLA Modules:
  0.0 103.9 jit_solution(12899579491343604535)
XLA Ops:
  0.6 100.7 %shard_map.50 = (bf16[8,16,16,128]{3,2,1,0:T(8,128)(2,1)}, f32[27,4,128]{2,1,0:T(4,128)}) custom-call(f32[27,4,128]{2,1,0:T(4,128)} %bitcast.3, bf16[8,16,16,128]{3,2,1,0:T(8,128)(2,1)} %in_hbm.1, bf16[8,16,16,128]{3,2,1,0:T(8,128)(2,1)} %cot_hbm.1), custom_call_target="tpu_custom_call" | custom-call | tf_op jit(solution)/shard_map/pallas_call | solution.py:351
  101.3 0.0 copy-start
  101.4 1.9 %copy.7 = bf16[8,16,16,128]{3,2,1,0:T(8,128)(2,1)} copy(bf16[8,16,16,128]{3,2,1,0:T(8,128)(2,1)} %get-tuple-element.8) | data formatting | bytes 1048576
  103.2 0.0 copy-done
  103.2 0.6 copy.8
Async XLA Ops:
  101.3 1.9 %copy-start = (f32[27,4,128]{2,1,0:T(4,128)S(1)}, f32[27,4,128]{2,1,0:T(4,128)}, u32[]{:S(2)}) copy-start(f32[27,4,128]{2,1,0:T(4,128)} %get-tuple-element.5) | copy-start | bytes 165892
where the time goes:
time: 104 us
  Pallas kernels  101 us (97%)
  local copies, waits for them, and re-layouts  2.51 us (2%)
    pallas_call x1, Pallas kernels, on_device(): pl.pallas_call(functools.partial(kernel, dims), out_shape=(jax.ShapeDtype...  101 us
    unnamed x4, local copies, waits for them, and re-layouts  2.51 us

commit v1 on v0

v1 whole, which is shorter than its diff:
```python
import functools

import jax
import jax.numpy as jnp
from jax import lax
from jax.experimental import pallas as pl
from jax.experimental.pallas import tpu as pltpu
from jax.sharding import PartitionSpec as P

var_eps = 1e-05
norm_eps = 1e-06
clip_norm = 600.0
F32 = jnp.float32
BF16 = jnp.bfloat16
MESH = pl.DeviceIdType.MESH
AXES = ("gx", "gy", "gz")

NCORE, NZL, NYC, NXC, NZH = 2, 4, 4, 4, 2
NZR = NZL * NZH
CHUNKS = ((0, 8, 2, 0), (8, 8, 2, 2), (16, 11, 3, 4))
SLOTS = 7


def kernel(raw_hbm, in_hbm, cot_hbm, dx_hbm, wg_ref, *scratch):
    (raw_ref, in_ref, shifted, face_out, edge_out, face_in, edge_in, corner_in, in_t, part, recv_c, send_xy, recv_xy,
     recv_z, full, std, wz, w_all, w_cat, dx_ref, stats_w, stats_g,
     load_sem, halo_send, halo_recv, c_send, c_recv, xy_send, xy_recv, z_send, z_recv, x_send, x_recv,
     w1_send, w1_recv, w2_send, w2_recv, w3_send, w3_recv, sw_send, sw_recv, sg_send, sg_recv) = scratch
    taps, rows, chan = raw_ref.shape
    ex, ey, ez = in_ref.shape[:3]
    fan_count = float(rows * NCORE * NZL * NYC * taps)
    count = {"gx": NCORE * NZL, "gy": NYC, "gz": NXC * NZH}
    me = {axis: lax.axis_index(axis) for axis in AXES}
    core, zl = lax.rem(me["gx"], NCORE), lax.div(me["gx"], NCORE)
    my = me["gy"]
    mx, zh = lax.rem(me["gz"], NXC), lax.div(me["gz"], NXC)
    mz = zh * NZL + zl

    def spot(c=None, x=None, y=None, z=None):
        c = core if c is None else c
        x = mx if x is None else x
        y = my if y is None else y
        z = mz if z is None else z
        return {"gx": lax.rem(z, NZL) * NCORE + c, "gy": y, "gz": lax.div(z, NZL) * NXC + x}

    partner = spot(c=1 - core)

    def plane_peer(k):
        flat = lax.rem(me["gx"] * NYC + my + k, 32)
        return {"gx": lax.div(flat, NYC), "gy": lax.rem(flat, NYC)}

    def xy_peer(k):
        flat = lax.rem(my * NXC + mx + k, NXC * NYC)
        return lax.rem(flat, NXC), lax.div(flat, NXC)

    flat_g = (my * NXC + mx) * NCORE + core

    def stat_peer(k):
        flat = lax.rem(flat_g + k, 32)
        where = lax.div(flat, NCORE)
        return spot(c=lax.rem(flat, NCORE), x=lax.rem(where, NXC), y=lax.div(where, NXC))

    def z_peer(k):
        return spot(z=lax.rem(mz + k, NZR))

    def remote(src, dst, send_sem, recv_sem, where):
        return pltpu.make_async_remote_copy(
            src_ref=src, dst_ref=dst, send_sem=send_sem, recv_sem=recv_sem,
            device_id=where, device_id_type=MESH,
        )

    sends = []

    def launch(copy):
        copy.start()
        sends.append(copy)
        return copy

    body = pl.ds(1, ey)
    load_cot = pltpu.make_async_copy(cot_hbm, shifted.at[1, pl.ds(1, ex), body], load_sem.at[0])
    load_raw = pltpu.make_async_copy(raw_hbm, raw_ref, load_sem.at[1])
    load_in = pltpu.make_async_copy(in_hbm, in_ref, load_sem.at[2])
    load_cot.start()
    load_raw.start()
    load_in.start()

    offsets = [(a, b, c) for c in (1, -1, 0) for a in (0, 1, -1) for b in (0, 1, -1) if (a, b, c) != (0, 0, 0)]

    def neighbour(off):
        return {axis: lax.rem(me[axis] + count[axis] + o, count[axis]) for axis, o in zip(AXES, off)}

    barrier = pltpu.get_barrier_semaphore()
    greeted = 0
    for off in offsets:
        if off[2] != 0:
            pl.semaphore_signal(barrier, inc=1, device_id=neighbour(off), device_id_type=MESH)
            greeted += 1
    for k in range(1, 32):
        pl.semaphore_signal(barrier, inc=1, device_id=plane_peer(k), device_id_type=MESH)
        pl.semaphore_signal(barrier, inc=1, device_id=stat_peer(k), device_id_type=MESH)
        greeted += 2
    for k in range(1, NZR):
        pl.semaphore_signal(barrier, inc=1, device_id=z_peer(k), device_id_type=MESH)
        greeted += 1

    low = {axis: me[axis] == 0 for axis in AXES}
    high = {axis: me[axis] == count[axis] - 1 for axis in AXES}
    tile = jnp.zeros((16, chan), BF16)
    for end, at_end in enumerate((low, high)):

        @pl.when(at_end["gx"])
        def _():
            shifted[1, (ex + 1) * end] = jnp.zeros((ey + 2, ez, chan), BF16)
            for side in range(2):
                face_in[side, (ex + 1) * end] = tile
                for b in range(2):
                    corner_in[side, b, end] = tile

        @pl.when(at_end["gy"])
        def _():
            shifted[1, :, (ey + 1) * end] = jnp.zeros((ex + 2, ez, chan), BF16)
            for side in range(2):
                edge_in[side, end] = tile
                for a in range(2):
                    corner_in[side, end, a] = tile

        @pl.when(at_end["gz"])
        def _():
            face_in[end] = jnp.zeros((ex + 2, ey, chan), BF16)
            edge_in[end] = jnp.zeros((2, 16, chan), BF16)
            corner_in[end] = jnp.zeros((2, 2, 16, chan), BF16)

    w_all[taps] = jnp.zeros((8, 16, chan), BF16)
    for y in range(NYC):
        send_xy[y, taps] = tile

    load_cot.wait()
    edge_rows = [[[], []], [[], []]]
    for x in range(ex):
        plane = shifted[1, x + 1, 1:ey + 1].astype(F32)
        for f, z in enumerate((0, ez - 1)):
            face = plane[:, z, :]
            face_out[f, x] = face.astype(BF16)
            edge_rows[f][0].append(face[0:1])
            edge_rows[f][1].append(face[ey - 1:ey])
    for f in range(2):
        for b in range(2):
            edge_out[f, b] = jnp.concatenate(edge_rows[f][b] + [jnp.zeros((16 - ex, chan), F32)], axis=0).astype(BF16)

    load_raw.wait()

    def per_output(value):
        return jnp.sum(jnp.sum(value, axis=0), axis=0, keepdims=True)

    raw = raw_ref[...]
    flat_w = me["gx"] * NYC + my
    stats_w[flat_w] = jnp.concatenate([per_output(raw), per_output(raw * raw), jnp.zeros((6, chan), F32)], axis=0)
    pl.semaphore_wait(barrier, greeted)

    def exists(off):
        ok = None
        for axis, o in zip(AXES, off):
            if o != 0:
                one = jnp.logical_not(high[axis] if o > 0 else low[axis])
                ok = one if ok is None else jnp.logical_and(ok, one)
        return ok

    def halo_copy(n, off):
        a, b, c = off
        near = {1: (ex, ey), -1: (1, 1)}
        if c == 0:
            xs = pl.ds(1, ex) if a == 0 else near[a][0]
            ys = body if b == 0 else near[b][1]
            xd = pl.ds(1, ex) if a == 0 else (0 if a > 0 else ex + 1)
            yd = body if b == 0 else (0 if b > 0 else ey + 1)
            src, dst = shifted.at[1, xs, ys], shifted.at[1, xd, yd]
        else:
            f, side = (1, 0) if c > 0 else (0, 1)
            if b == 0:
                xs = pl.ds(0, ex) if a == 0 else (ex - 1 if a > 0 else 0)
                xd = pl.ds(1, ex) if a == 0 else (0 if a > 0 else ex + 1)
                src, dst = face_out.at[f, xs], face_in.at[side, xd]
            else:
                src = edge_out.at[f, 1 if b > 0 else 0]
                ys = 0 if b > 0 else 1
                dst = edge_in.at[side, ys] if a == 0 else corner_in.at[side, ys, 0 if a > 0 else 1]
        return remote(src, dst, halo_send.at[n], halo_recv.at[n], neighbour(off))

    halos = [(off, halo_copy(n, off)) for n, off in enumerate(offsets)]
    for off, copy in halos:

        @pl.when(exists(off))
        def _():
            copy.start()

    def halo_wait(keep):
        for off, copy in halos:
            if keep(off):

                @pl.when(exists(tuple(-o for o in off)))
                def _():
                    copy.wait_recv()

    weight_sums = [
        launch(remote(stats_w.at[flat_w], stats_w.at[flat_w], sw_send.at[k - 1], sw_recv.at[k - 1], plane_peer(k)))
        for k in range(1, 32)
    ]

    row_i = lax.broadcasted_iota(jnp.int32, (chan, chan), 0)
    col_i = lax.broadcasted_iota(jnp.int32, (chan, chan), 1)

    def natural(i):
        return (i // 4 % 4) * 32 + (i // 64) * 16 + (i // 16 % 4) * 4 + i % 4

    to_mine = jnp.where(col_i == natural(row_i), 1.0, 0.0).astype(BF16)
    to_natural = jnp.where(row_i == natural(col_i), 1.0, 0.0).astype(BF16)

    load_in.wait()
    for x in range(ex):
        block = in_ref[x].reshape(ey * ez, chan)
        in_t[:, x * ey * ez:(x + 1) * ey * ez] = lax.dot_general(
            to_mine, block, (((1,), (1,)), ((), ())), preferred_element_type=F32
        ).astype(BF16)

    order = [t for c in (1, 0, 2) for t in range(c, taps, 3)]

    def view(t, start, planes):
        a, b, c = t // 9, (t // 3) % 3, t % 3
        block = shifted[2 - c, pl.ds(start + 2 - a, planes), 2 - b:2 - b + ey]
        return block.reshape(planes * ey * ez, chan)

    half_rows = chan // NCORE

    def filter_chunk(n):
        first, done, _, _ = CHUNKS[n]
        for u in range(first, first + done, 2):
            group = list(range(u, min(u + 2, first + done)))
            views = [view(order[v], 0, ex) for v in group]
            right = jnp.concatenate(views, axis=1) if len(views) > 1 else views[0]
            product = jnp.dot(in_t[...], right, preferred_element_type=F32)
            for j, v in enumerate(group):
                for c in range(NCORE):
                    part[c, v] = product[c * half_rows:(c + 1) * half_rows, j * chan:(j + 1) * chan]
        span = pl.ds(first, done)
        return launch(remote(part.at[1 - core, span], recv_c.at[span], c_send.at[n], c_recv.at[n], partner))

    def xy_chunk(n, copy):
        first, done, each, slot = CHUNKS[n]
        copy.wait_recv()
        for v in range(first, first + done):
            total = part[core, v] + recv_c[v]
            for y in range(NYC):
                send_xy[y, v] = total[y * 16:(y + 1) * 16].astype(BF16)
        copies = []
        for k in range(1, NXC * NYC):
            px, py = xy_peer(k)
            index = n * 15 + k - 1
            copies.append(launch(remote(
                send_xy.at[py, pl.ds(first + px * each, each)], recv_xy.at[k - 1, pl.ds(slot, each)],
                xy_send.at[index], xy_recv.at[index], spot(x=px, y=py),
            )))
        return copies

    def z_chunk(n, copies):
        first, done, each, slot = CHUNKS[n]
        for copy in copies:
            copy.wait_recv()
        span = pl.ds(slot, each)
        total = send_xy[my, pl.ds(first + mx * each, each)].astype(F32)
        for k in range(1, NXC * NYC):
            total = total + recv_xy[k - 1, span].astype(F32)
        recv_z[mz, span] = total.astype(BF16)
        return [
            launch(remote(recv_z.at[mz, span], recv_z.at[mz, span],
                          z_send.at[n * 7 + k - 1], z_recv.at[n * 7 + k - 1], z_peer(k)))
            for k in range(1, NZR)
        ]

    def shift(slot, side, amount, edge):
        depth = lax.broadcasted_iota(jnp.int32, (ey, ez, chan), 1)
        for x in range(ex + 2):
            plane = shifted[1, x, 1:ey + 1].astype(F32)
            outer = face_in[side, x].astype(F32)[:, None, :]
            shifted[slot, x, 1:ey + 1] = jnp.where(depth == edge, outer, pltpu.roll(plane, amount, 1)).astype(BF16)
        depth = lax.broadcasted_iota(jnp.int32, (ex + 2, ez, chan), 1)
        for b in range(2):
            y = (ey + 1) * b
            plane = shifted[1, :, y].astype(F32)
            outer = jnp.concatenate([
                corner_in[side, b, 0].astype(F32)[ex - 1:ex], edge_in[side, b].astype(F32)[0:ex],
                corner_in[side, b, 1].astype(F32)[0:1],
            ], axis=0)[:, None, :]
            shifted[slot, :, y] = jnp.where(depth == edge, outer, pltpu.roll(plane, amount, 1)).astype(BF16)

    halo_wait(lambda off: off[2] == 0)
    core_0 = filter_chunk(0)

    for copy in weight_sums:
        copy.wait_recv()
    sums = stats_w[0]
    for k in range(1, 32):
        sums = sums + stats_w[k]
    mean_out = sums[0:1] / fan_count
    var_out = sums[1:2] / fan_count - mean_out * mean_out
    inv_std = lax.rsqrt(var_out + var_eps)
    for u, t in enumerate(order):
        value = (raw_ref[t] - mean_out) * inv_std
        std[u] = value
        wz[zl, u] = value.astype(BF16)
    gather_z = [
        launch(remote(wz.at[zl], wz.at[zl], w1_send.at[k - 1], w1_recv.at[k - 1], spot(z=zh * NZL + lax.rem(zl + k, NZL))))
        for k in range(1, NZL)
    ]

    xy_0 = xy_chunk(0, core_0)
    halo_wait(lambda off: off[2] == -1)
    shift(2, 1, ez - 1, ez - 1)
    core_1 = filter_chunk(1)
    halo_wait(lambda off: off[2] == 1)
    shift(0, 0, 1, 0)
    xy_1 = xy_chunk(1, core_1)
    core_2 = filter_chunk(2)

    for copy in gather_z:
        copy.wait_recv()
    slab = core * NYC + my
    for u in range(taps):
        w_all[u, slab] = wz[:, u].astype(F32).reshape(16, chan).astype(BF16)
    xy_2 = xy_chunk(2, core_2)
    gather_y = [
        launch(remote(w_all.at[pl.ds(0, taps), slab], w_all.at[pl.ds(0, taps), slab],
                      w2_send.at[k - 1], w2_recv.at[k - 1], spot(y=lax.rem(my + k, NYC))))
        for k in range(1, NYC)
    ]
    z_0 = z_chunk(0, xy_0)
    z_1 = z_chunk(1, xy_1)
    z_2 = z_chunk(2, xy_2)
    for copy in gather_y:
        copy.wait_recv()
    slabs = w_all.at[pl.ds(0, taps), pl.ds(core * NYC, NYC)]
    gather_c = launch(remote(slabs, slabs, w3_send.at[0], w3_recv.at[0], partner))

    gather_c.wait_recv()
    for u in range(0, taps, 2):
        group = range(u, min(u + 2, taps))
        right = [w_all[v].reshape(chan, chan) for v in group]
        right = jnp.concatenate(right, axis=1) if len(right) > 1 else right[0]
        w_cat[:, u * chan:(u + len(group)) * chan] = jnp.dot(
            to_natural, right, preferred_element_type=F32
        ).astype(BF16)
    step = 2
    half = ex // 2

    def dx_step(n, carry):
        start = n * step
        left = jnp.concatenate([view(t, start, step) for t in order], axis=1)
        product = lax.dot_general(left, w_cat[...], (((1,), (1,)), ((), ())), preferred_element_type=F32)
        dx_ref[pl.ds(start, step)] = product.astype(BF16).reshape(step, ey, ez, chan)
        return carry

    stores = [
        pltpu.make_async_copy(dx_ref.at[pl.ds(h * half, half)], dx_hbm.at[pl.ds(h * half, half)], load_sem.at[3 + h])
        for h in range(2)
    ]
    lax.fori_loop(0, half // step, dx_step, 0)
    stores[0].start()

    for copy in z_0 + z_1 + z_2:
        copy.wait_recv()
    grad = recv_z[0].astype(F32)
    for k in range(1, NZR):
        grad = grad + recv_z[k].astype(F32)
    near = []
    for first, _, each, _ in CHUNKS:
        near += [w_all[first + mx * each + j, slab].astype(F32) for j in range(each)]
    cross = grad[0] * near[0]
    for j in range(1, SLOTS):
        cross = cross + grad[j] * near[j]
    stats_g[flat_g] = jnp.concatenate(
        [per_output(grad), jnp.sum(cross, axis=0, keepdims=True), per_output(grad * grad), jnp.zeros((5, chan), F32)],
        axis=0,
    )
    grad_sums = [
        launch(remote(stats_g.at[flat_g], stats_g.at[flat_g], sg_send.at[k - 1], sg_recv.at[k - 1], stat_peer(k)))
        for k in range(1, 32)
    ]
    for j in range(SLOTS):
        mine = grad[j, 0:rows]
        for q in range(1, NZL):
            mine = jnp.where(zl == q, grad[j, q * rows:(q + 1) * rows], mine)
        full[mx, j] = mine
    gather_x = [
        launch(remote(full.at[mx], full.at[mx], x_send.at[k - 1], x_recv.at[k - 1], spot(x=lax.rem(mx + k, NXC))))
        for k in range(1, NXC)
    ]

    lax.fori_loop(half // step, ex // step, dx_step, 0)
    stores[1].start()

    for copy in gather_x + grad_sums:
        copy.wait_recv()
    sums = stats_g[0]
    for k in range(1, 32):
        sums = sums + stats_g[k]
    sum_grad, sum_cross, sum_square = sums[0:1], sums[1:2], sums[2:3]
    mean_grad = sum_grad / fan_count
    mean_cross = sum_cross / fan_count
    spread = sum_square - 2.0 * mean_grad * sum_grad - 2.0 * mean_cross * sum_cross
    spread = (
        spread
        + fan_count * mean_grad * mean_grad
        + fan_count * mean_cross * mean_cross * var_out / (var_out + var_eps)
    )
    square_sum = jnp.sum(inv_std * inv_std * spread, axis=1, keepdims=True)
    scale = jnp.minimum(1.0, clip_norm * lax.rsqrt(square_sum + norm_eps))
    factor = inv_std * scale
    for first, done, each, slot in CHUNKS:
        for v in range(done):
            u = first + v
            wg_ref[order[u]] = factor * (full[v // each, slot + v % each] - mean_grad - std[u] * mean_cross)

    for copy in sends:
        copy.wait_send()
    for off, copy in halos:

        @pl.when(exists(off))
        def _():
            copy.wait_send()
    for copy in stores:
        copy.wait()


def on_device(raw_weight, inputs, cotangent):
    rows, taps, chan = raw_weight.shape
    ex, ey, ez = inputs.shape[:3]
    dma = pltpu.SemaphoreType.DMA

    def pair(n):
        return [dma((n,)), dma((n,))]

    scratch = [
        pltpu.VMEM((taps, rows, chan), F32),
        pltpu.VMEM(inputs.shape, BF16),
        pltpu.VMEM((3, ex + 2, ey + 2, ez, chan), BF16),
        pltpu.VMEM((2, ex, ey, chan), BF16),
        pltpu.VMEM((2, 2, 16, chan), BF16),
        pltpu.VMEM((2, ex + 2, ey, chan), BF16),
        pltpu.VMEM((2, 2, 16, chan), BF16),
        pltpu.VMEM((2, 2, 2, 16, chan), BF16),
        pltpu.VMEM((chan, ex * ey * ez), BF16),
        pltpu.VMEM((NCORE, taps, chan // NCORE, chan), F32),
        pltpu.VMEM((taps, chan // NCORE, chan), F32),
        pltpu.VMEM((NYC, taps + 1, 16, chan), BF16),
        pltpu.VMEM((NXC * NYC - 1, SLOTS, 16, chan), BF16),
        pltpu.VMEM((NZR, SLOTS, 16, chan), BF16),
        pltpu.VMEM((NXC, SLOTS, rows, chan), F32),
        pltpu.VMEM((taps, rows, chan), F32),
        pltpu.VMEM((NZL, taps, rows, chan), BF16),
        pltpu.VMEM((taps + 1, 8, 16, chan), BF16),
        pltpu.VMEM((chan, taps * chan), BF16),
        pltpu.VMEM(inputs.shape, BF16),
        pltpu.VMEM((32, 8, chan), F32),
        pltpu.VMEM((32, 8, chan), F32),
        dma((5,)), *pair(26), *pair(3), *pair(45), *pair(21), *pair(3),
        *pair(3), *pair(3), *pair(1), *pair(31), *pair(31),
    ]
    vmem = pl.BlockSpec(memory_space=pltpu.VMEM)
    anywhere = pl.BlockSpec(memory_space=pl.ANY)
    input_grad, weight_grad = pl.pallas_call(
        kernel,
        out_shape=(
            jax.ShapeDtypeStruct(cotangent.shape, BF16),
            jax.ShapeDtypeStruct((taps, rows, chan), F32),
        ),
        in_specs=[anywhere] * 3,
        out_specs=(anywhere, vmem),
        scratch_shapes=scratch,
        compiler_params=pltpu.CompilerParams(
            collective_id=0, has_side_effects=True, vmem_limit_bytes=60 * 1024 * 1024
        ),
    )(jnp.transpose(raw_weight, (1, 0, 2)), inputs, cotangent)
    return input_grad, jnp.transpose(weight_grad, (1, 0, 2))


def solution(mesh):
    in_specs = (P(("gx", "gy"), None, None), P("gx", "gy", "gz", None), P("gx", "gy", "gz", None))
    out_specs = (P("gx", "gy", "gz", None), P(("gx", "gy"), None, None))
    return jax.shard_map(
        on_device, mesh=mesh, in_specs=in_specs, out_specs=out_specs, check_vma=False
    )
```

time: 104 us -> 50.2 us (0.48)
  Pallas kernels: 101 us -> 46.9 us
    pallas_call x1, Pallas kernels: 101 us -> 46.9 us  [on_device(): pl.pallas_call(kernel, out_shape=(jax.ShapeDtypeStruct(cotangent.shape, B...]
where the time goes in v1:
time: 50.2 us; the launch traced here: 50.1 us
  Pallas kernels  46.9 us (93%)
  local copies, waits for them, and re-layouts  2.51 us (5%)
  between operations  0.65 us (1%)
    pallas_call x1, Pallas kernels, on_device(): pl.pallas_call(kernel, out_shape=(jax.ShapeDtypeStruct(cotangent.shape, B...  46.9 us
    unnamed x4, local copies, waits for them, and re-layouts  2.51 us

profile of v1, /device:TPU:1, one launch (start us, length us, event | category | flops | bytes accessed | tf_op | source)
XLA Modules:
  0.0 50.1 jit_solution(5268983886781304999)
XLA Ops:
  0.6 46.9 %shard_map.50 = (bf16[8,16,16,128]{3,2,1,0:T(8,128)(2,1)}, f32[27,4,128]{2,1,0:T(4,128)}) custom-call(f32[27,4,128]{2,1,0:T(4,128)} %bitcast.3, bf16[8,16,16,128]{3,2,1,0:T(8,128)(2,1)} %in_hbm.1, bf16[8,16,16,128]{3,2,1,0:T(8,128)(2,1)} %cot_hbm.1), custom_call_target="tpu_custom_call" | custom-call | tf_op jit(solution)/shard_map/pallas_call | solution.py:469
  47.6 0.0 copy-start
  47.6 1.9 %copy.7 = bf16[8,16,16,128]{3,2,1,0:T(8,128)(2,1)} copy(bf16[8,16,16,128]{3,2,1,0:T(8,128)(2,1)} %get-tuple-element.8) | data formatting | bytes 1048576
  49.5 0.0 copy-done
  49.5 0.6 %copy.8 = f32[4,27,128]{2,0,1:T(4,128)} copy(f32[4,27,128]{2,0,1:T(4,128)S(1)} %bitcast.2) | data formatting | bytes 110592
Async XLA Ops:
  47.6 1.9 %copy-start = (f32[27,4,128]{2,1,0:T(4,128)S(1)}, f32[27,4,128]{2,1,0:T(4,128)}, u32[]{:S(2)}) copy-start(f32[27,4,128]{2,1,0:T(4,128)} %get-tuple-element.5) | copy-start | bytes 165892

commit v2 on v1

--- a/solution.py
+++ b/solution.py
@@ -21,11 +21,9 @@
 SLOTS = 7
 
 
-def kernel(raw_hbm, in_hbm, cot_hbm, dx_hbm, wg_ref, *scratch):
+def kernel(raw_hbm, in_hbm, cot_hbm, dx_ref, wg_ref, *scratch):
     (raw_ref, in_ref, shifted, face_out, edge_out, face_in, edge_in, corner_in, in_t, part, recv_c, send_xy, recv_xy,
-     recv_z, full, std, wz, w_all, w_cat, dx_ref, stats_w, stats_g,
-     load_sem, halo_send, halo_recv, c_send, c_recv, xy_send, xy_recv, z_send, z_recv, x_send, x_recv,
-     w1_send, w1_recv, w2_send, w2_recv, w3_send, w3_recv, sw_send, sw_recv, sg_send, sg_recv) = scratch
+     recv_z, full, std, wz, w_all, w_cat, stats_w, stats_g, load_sem, halo_send, halo_recv, sems) = scratch
     taps, rows, chan = raw_ref.shape
     ex, ey, ez = in_ref.shape[:3]
     fan_count = float(rows * NCORE * NZL * NYC * taps)
@@ -69,12 +67,14 @@
             device_id=where, device_id_type=MESH,
         )
 
-    sends = []
-
-    def launch(copy):
-        copy.start()
-        sends.append(copy)
-        return copy
+    pending = []
+
+    def group(copies, whole, send_sem, recv_sem):
+        for src, dst, where in copies:
+            remote(src, dst, send_sem, recv_sem, where).start()
+        total = remote(whole, whole, send_sem, recv_sem, partner)
+        pending.append(total)
+        return total
 
     body = pl.ds(1, ey)
     load_cot = pltpu.make_async_copy(cot_hbm, shifted.at[1, pl.ds(1, ex), body], load_sem.at[0])
@@ -97,10 +97,16 @@
             greeted += 1
     for k in range(1, 32):
         pl.semaphore_signal(barrier, inc=1, device_id=plane_peer(k), device_id_type=MESH)
-        pl.semaphore_signal(barrier, inc=1, device_id=stat_peer(k), device_id_type=MESH)
-        greeted += 2
-    for k in range(1, NZR):
-        pl.semaphore_signal(barrier, inc=1, device_id=z_peer(k), device_id_type=MESH)
+        greeted += 1
+    for dx in range(1, NXC):
+        for dy in range(NYC):
+            for c in range(NCORE):
+                where = spot(c=c, x=lax.rem(mx + dx, NXC), y=lax.rem(my + dy, NYC))
+                pl.semaphore_signal(barrier, inc=1, device_id=where, device_id_type=MESH)
+                greeted += 1
+    for k in range(NZL):
+        where = spot(z=(1 - zh) * NZL + lax.rem(zl + k, NZL))
+        pl.semaphore_signal(barrier, inc=1, device_id=where, device_id_type=MESH)
         greeted += 1
 
     low = {axis: me[axis] == 0 for axis in AXES}
@@ -134,7 +140,8 @@
     for y in range(NYC):
         send_xy[y, taps] = tile
 
-    load_cot.wait()
+    with jax.named_scope('w_cot'):
+        load_cot.wait()
     edge_rows = [[[], []], [[], []]]
     for x in range(ex):
         plane = shifted[1, x + 1, 1:ey + 1].astype(F32)
@@ -154,8 +161,9 @@
 
     raw = raw_ref[...]
     flat_w = me["gx"] * NYC + my
-    stats_w[flat_w] = jnp.concatenate([per_output(raw), per_output(raw * raw), jnp.zeros((6, chan), F32)], axis=0)
-    pl.semaphore_wait(barrier, greeted)
+    stats_w[flat_w] = jnp.concatenate([per_output(raw), per_output(raw * raw)], axis=0)
+    with jax.named_scope("w_barrier"):
+        pl.semaphore_wait(barrier, greeted)
 
     def exists(off):
         ok = None
@@ -201,10 +209,10 @@
                 def _():
                     copy.wait_recv()
 
-    weight_sums = [
-        launch(remote(stats_w.at[flat_w], stats_w.at[flat_w], sw_send.at[k - 1], sw_recv.at[k - 1], plane_peer(k)))
-        for k in range(1, 32)
-    ]
+    weight_sums = group(
+        [(stats_w.at[flat_w], stats_w.at[flat_w], plane_peer(k)) for k in range(1, 32)],
+        stats_w.at[pl.ds(0, 31)], sems.at[0], sems.at[1],
+    )
 
     row_i = lax.broadcasted_iota(jnp.int32, (chan, chan), 0)
     col_i = lax.broadcasted_iota(jnp.int32, (chan, chan), 1)
@@ -234,19 +242,22 @@
     def filter_chunk(n):
         first, done, _, _ = CHUNKS[n]
         for u in range(first, first + done, 2):
-            group = list(range(u, min(u + 2, first + done)))
-            views = [view(order[v], 0, ex) for v in group]
+            both = list(range(u, min(u + 2, first + done)))
+            views = [view(order[v], 0, ex) for v in both]
             right = jnp.concatenate(views, axis=1) if len(views) > 1 else views[0]
             product = jnp.dot(in_t[...], right, preferred_element_type=F32)
-            for j, v in enumerate(group):
+            for j, v in enumerate(both):
                 for c in range(NCORE):
                     part[c, v] = product[c * half_rows:(c + 1) * half_rows, j * chan:(j + 1) * chan]
         span = pl.ds(first, done)
-        return launch(remote(part.at[1 - core, span], recv_c.at[span], c_send.at[n], c_recv.at[n], partner))
+        return group(
+            [(part.at[1 - core, span], recv_c.at[span], partner)], recv_c.at[span], sems.at[2 + n], sems.at[5 + n]
+        )
 
     def xy_chunk(n, copy):
         first, done, each, slot = CHUNKS[n]
-        copy.wait_recv()
+        with jax.named_scope("w_core%d" % n):
+            copy.wait_recv()
         for v in range(first, first + done):
             total = part[core, v] + recv_c[v]
             for y in range(NYC):
@@ -254,27 +265,25 @@
         copies = []
         for k in range(1, NXC * NYC):
             px, py = xy_peer(k)
-            index = n * 15 + k - 1
-            copies.append(launch(remote(
+            copies.append((
                 send_xy.at[py, pl.ds(first + px * each, each)], recv_xy.at[k - 1, pl.ds(slot, each)],
-                xy_send.at[index], xy_recv.at[index], spot(x=px, y=py),
-            )))
-        return copies
-
-    def z_chunk(n, copies):
+                spot(x=px, y=py),
+            ))
+        return group(copies, recv_xy.at[:, pl.ds(slot, each)], sems.at[8 + n], sems.at[11 + n])
+
+    def z_chunk(n, copy):
         first, done, each, slot = CHUNKS[n]
-        for copy in copies:
+        with jax.named_scope("w_xy%d" % n):
             copy.wait_recv()
         span = pl.ds(slot, each)
         total = send_xy[my, pl.ds(first + mx * each, each)].astype(F32)
         for k in range(1, NXC * NYC):
             total = total + recv_xy[k - 1, span].astype(F32)
         recv_z[mz, span] = total.astype(BF16)
-        return [
-            launch(remote(recv_z.at[mz, span], recv_z.at[mz, span],
-                          z_send.at[n * 7 + k - 1], z_recv.at[n * 7 + k - 1], z_peer(k)))
-            for k in range(1, NZR)
-        ]
+        return group(
+            [(recv_z.at[mz, span], recv_z.at[mz, span], z_peer(k)) for k in range(1, NZR)],
+            recv_z.at[pl.ds(0, NZR - 1), span], sems.at[14 + n], sems.at[17 + n],
+        )
 
     def shift(slot, side, amount, edge):
         depth = lax.broadcasted_iota(jnp.int32, (ey, ez, chan), 1)
@@ -292,11 +301,23 @@
             ], axis=0)[:, None, :]
             shifted[slot, :, y] = jnp.where(depth == edge, outer, pltpu.roll(plane, amount, 1)).astype(BF16)
 
-    halo_wait(lambda off: off[2] == 0)
+    with jax.named_scope("w_halo_xy"):
+        halo_wait(lambda off: off[2] == 0)
     core_0 = filter_chunk(0)
-
-    for copy in weight_sums:
-        copy.wait_recv()
+    with jax.named_scope("w_halo_z1"):
+        halo_wait(lambda off: off[2] == -1)
+    shift(2, 1, ez - 1, ez - 1)
+    core_1 = filter_chunk(1)
+    xy_0 = xy_chunk(0, core_0)
+    with jax.named_scope("w_halo_z2"):
+        halo_wait(lambda off: off[2] == 1)
+    shift(0, 0, 1, 0)
+    core_2 = filter_chunk(2)
+    xy_1 = xy_chunk(1, core_1)
+    xy_2 = xy_chunk(2, core_2)
+
+    with jax.named_scope("w_weight_sums"):
+        weight_sums.wait_recv()
     sums = stats_w[0]
     for k in range(1, 32):
         sums = sums + stats_w[k]
@@ -307,66 +328,33 @@
         value = (raw_ref[t] - mean_out) * inv_std
         std[u] = value
         wz[zl, u] = value.astype(BF16)
-    gather_z = [
-        launch(remote(wz.at[zl], wz.at[zl], w1_send.at[k - 1], w1_recv.at[k - 1], spot(z=zh * NZL + lax.rem(zl + k, NZL))))
-        for k in range(1, NZL)
-    ]
-
-    xy_0 = xy_chunk(0, core_0)
-    halo_wait(lambda off: off[2] == -1)
-    shift(2, 1, ez - 1, ez - 1)
-    core_1 = filter_chunk(1)
-    halo_wait(lambda off: off[2] == 1)
-    shift(0, 0, 1, 0)
-    xy_1 = xy_chunk(1, core_1)
-    core_2 = filter_chunk(2)
-
-    for copy in gather_z:
-        copy.wait_recv()
+    gather_z = group(
+        [(wz.at[zl], wz.at[zl], spot(z=zh * NZL + lax.rem(zl + k, NZL))) for k in range(1, NZL)],
+        wz.at[pl.ds(0, NZL - 1)], sems.at[20], sems.at[21],
+    )
+
+    z_0 = z_chunk(0, xy_0)
+    with jax.named_scope("w_gather_z"):
+        gather_z.wait_recv()
     slab = core * NYC + my
     for u in range(taps):
         w_all[u, slab] = wz[:, u].astype(F32).reshape(16, chan).astype(BF16)
-    xy_2 = xy_chunk(2, core_2)
-    gather_y = [
-        launch(remote(w_all.at[pl.ds(0, taps), slab], w_all.at[pl.ds(0, taps), slab],
-                      w2_send.at[k - 1], w2_recv.at[k - 1], spot(y=lax.rem(my + k, NYC))))
-        for k in range(1, NYC)
-    ]
-    z_0 = z_chunk(0, xy_0)
+    tap_span = pl.ds(0, taps)
+    gather_y = group(
+        [(w_all.at[tap_span, slab], w_all.at[tap_span, slab], spot(y=lax.rem(my + k, NYC))) for k in range(1, NYC)],
+        w_all.at[tap_span, pl.ds(0, NYC - 1)], sems.at[22], sems.at[23],
+    )
     z_1 = z_chunk(1, xy_1)
     z_2 = z_chunk(2, xy_2)
-    for copy in gather_y:
-        copy.wait_recv()
-    slabs = w_all.at[pl.ds(0, taps), pl.ds(core * NYC, NYC)]
-    gather_c = launch(remote(slabs, slabs, w3_send.at[0], w3_recv.at[0], partner))
-
-    gather_c.wait_recv()
-    for u in range(0, taps, 2):
-        group = range(u, min(u + 2, taps))
-        right = [w_all[v].reshape(chan, chan) for v in group]
-        right = jnp.concatenate(right, axis=1) if len(right) > 1 else right[0]
-        w_cat[:, u * chan:(u + len(group)) * chan] = jnp.dot(
-            to_natural, right, preferred_element_type=F32
-        ).astype(BF16)
-    step = 2
-    half = ex // 2
-
-    def dx_step(n, carry):
-        start = n * step
-        left = jnp.concatenate([view(t, start, step) for t in order], axis=1)
-        product = lax.dot_general(left, w_cat[...], (((1,), (1,)), ((), ())), preferred_element_type=F32)
-        dx_ref[pl.ds(start, step)] = product.astype(BF16).reshape(step, ey, ez, chan)
-        return carry
-
-    stores = [
-        pltpu.make_async_copy(dx_ref.at[pl.ds(h * half, half)], dx_hbm.at[pl.ds(h * half, half)], load_sem.at[3 + h])
-        for h in range(2)
-    ]
-    lax.fori_loop(0, half // step, dx_step, 0)
-    stores[0].start()
-
-    for copy in z_0 + z_1 + z_2:
-        copy.wait_recv()
+    with jax.named_scope("w_gather_y"):
+        gather_y.wait_recv()
+    slabs = w_all.at[tap_span, pl.ds(core * NYC, NYC)]
+    gather_c = group([(slabs, slabs, partner)], slabs, sems.at[24], sems.at[25])
+
+    with jax.named_scope("w_z"):
+        z_0.wait_recv()
+        z_1.wait_recv()
+        z_2.wait_recv()
     grad = recv_z[0].astype(F32)
     for k in range(1, NZR):
         grad = grad + recv_z[k].astype(F32)
@@ -377,28 +365,48 @@
     for j in range(1, SLOTS):
         cross = cross + grad[j] * near[j]
     stats_g[flat_g] = jnp.concatenate(
-        [per_output(grad), jnp.sum(cross, axis=0, keepdims=True), per_output(grad * grad), jnp.zeros((5, chan), F32)],
+        [per_output(grad), jnp.sum(cross, axis=0, keepdims=True), per_output(grad * grad), jnp.zeros((1, chan), F32)],
         axis=0,
     )
-    grad_sums = [
-        launch(remote(stats_g.at[flat_g], stats_g.at[flat_g], sg_send.at[k - 1], sg_recv.at[k - 1], stat_peer(k)))
-        for k in range(1, 32)
-    ]
+    grad_sums = group(
+        [(stats_g.at[flat_g], stats_g.at[flat_g], stat_peer(k)) for k in range(1, 32)],
+        stats_g.at[pl.ds(0, 31)], sems.at[26], sems.at[27],
+    )
     for j in range(SLOTS):
         mine = grad[j, 0:rows]
         for q in range(1, NZL):
             mine = jnp.where(zl == q, grad[j, q * rows:(q + 1) * rows], mine)
         full[mx, j] = mine
-    gather_x = [
-        launch(remote(full.at[mx], full.at[mx], x_send.at[k - 1], x_recv.at[k - 1], spot(x=lax.rem(mx + k, NXC))))
-        for k in range(1, NXC)
-    ]
-
-    lax.fori_loop(half // step, ex // step, dx_step, 0)
-    stores[1].start()
-
-    for copy in gather_x + grad_sums:
-        copy.wait_recv()
+    gather_x = group(
+        [(full.at[mx], full.at[mx], spot(x=lax.rem(mx + k, NXC))) for k in range(1, NXC)],
+        full.at[pl.ds(0, NXC - 1)], sems.at[28], sems.at[29],
+    )
+
+    with jax.named_scope("w_gather_c"):
+        gather_c.wait_recv()
+    for u in range(0, taps, 2):
+        pair = range(u, min(u + 2, taps))
+        right = [w_all[v].reshape(chan, chan) for v in pair]
+        right = jnp.concatenate(right, axis=1) if len(right) > 1 else right[0]
+        w_cat[:, u * chan:(u + len(pair)) * chan] = jnp.dot(
+            to_natural, right, preferred_element_type=F32
+        ).astype(BF16)
+    step = 2
+
+    def dx_step(n, carry):
+        start = n * step
+        left = jnp.concatenate([view(t, start, step) for t in order], axis=1)
+        product = lax.dot_general(left, w_cat[...], (((1,), (1,)), ((), ())), preferred_element_type=F32)
+        dx_ref[pl.ds(start, step)] = product.astype(BF16).reshape(step, ey, ez, chan)
+        return carry
+
+    with jax.named_scope("dx"):
+        lax.fori_loop(0, ex // step, dx_step, 0)
+
+    with jax.named_scope("w_grad_sums"):
+        grad_sums.wait_recv()
+    with jax.named_scope("w_gather_x"):
+        gather_x.wait_recv()
     sums = stats_g[0]
     for k in range(1, 32):
         sums = sums + stats_g[k]
@@ -419,14 +427,21 @@
             u = first + v
             wg_ref[order[u]] = factor * (full[v // each, slot + v % each] - mean_grad - std[u] * mean_cross)
 
-    for copy in sends:
-        copy.wait_send()
+    with jax.named_scope("w_sends"):
+        for copy in pending:
+            copy.wait_send()
     for off, copy in halos:
 
         @pl.when(exists(off))
         def _():
             copy.wait_send()
-    for copy in stores:
+
+
+def write_out(dx_ref, wg_ref, dx_hbm, wg_hbm, sem):
+    copies = [pltpu.make_async_copy(dx_ref, dx_hbm, sem.at[0]), pltpu.make_async_copy(wg_ref, wg_hbm, sem.at[1])]
+    for copy in copies:
+        copy.start()
+    for copy in copies:
         copy.wait()
 
 
@@ -434,9 +449,6 @@
     rows, taps, chan = raw_weight.shape
     ex, ey, ez = inputs.shape[:3]
     dma = pltpu.SemaphoreType.DMA
-
-    def pair(n):
-        return [dma((n,)), dma((n,))]
 
     scratch = [
         pltpu.VMEM((taps, rows, chan), F32),
@@ -458,27 +470,36 @@
         pltpu.VMEM((NZL, taps, rows, chan), BF16),
         pltpu.VMEM((taps + 1, 8, 16, chan), BF16),
         pltpu.VMEM((chan, taps * chan), BF16),
-        pltpu.VMEM(inputs.shape, BF16),
-        pltpu.VMEM((32, 8, chan), F32),
-        pltpu.VMEM((32, 8, chan), F32),
-        dma((5,)), *pair(26), *pair(3), *pair(45), *pair(21), *pair(3),
-        *pair(3), *pair(3), *pair(1), *pair(31), *pair(31),
+        pltpu.VMEM((32, 2, chan), F32),
+        pltpu.VMEM((32, 4, chan), F32),
+        dma((3,)), dma((26,)), dma((26,)), dma((30,)),
     ]
     vmem = pl.BlockSpec(memory_space=pltpu.VMEM)
     anywhere = pl.BlockSpec(memory_space=pl.ANY)
-    input_grad, weight_grad = pl.pallas_call(
+    shapes = (
+        jax.ShapeDtypeStruct(cotangent.shape, BF16),
+        jax.ShapeDtypeStruct((taps, rows, chan), F32),
+    )
+    results = pl.pallas_call(
         kernel,
-        out_shape=(
-            jax.ShapeDtypeStruct(cotangent.shape, BF16),
-            jax.ShapeDtypeStruct((taps, rows, chan), F32),
-        ),
+        out_shape=tuple(pltpu.VMEM(one.shape, one.dtype) for one in shapes),
         in_specs=[anywhere] * 3,
-        out_specs=(anywhere, vmem),
+        out_specs=(vmem, vmem),
         scratch_shapes=scratch,
         compiler_params=pltpu.CompilerParams(
-            collective_id=0, has_side_effects=True, vmem_limit_bytes=60 * 1024 * 1024
+            collective_id=0, has_side_effects=True, vmem_limit_bytes=32 * 1024 * 1024
         ),
-    )(jnp.transpose(raw_weight, (1, 0, 2)), inputs, cotangent)
+    )(*(
+        pltpu.with_memory_space_constraint(one, pltpu.HBM)
+        for one in (jnp.transpose(raw_weight, (1, 0, 2)), inputs, cotangent)
+    ))
+    input_grad, weight_grad = pl.pallas_call(
+        write_out,
+        out_shape=shapes,
+        in_specs=[vmem, vmem],
+        out_specs=(anywhere, anywhere),
+        scratch_shapes=[dma((2,))],
+    )(*(pltpu.with_memory_space_constraint(one, pltpu.VMEM) for one in results))
     return input_grad, jnp.transpose(weight_grad, (1, 0, 2))
 
 

time: 50.2 us -> 41.9 us (0.83)
  Pallas kernels: 46.9 us -> 41.2 us
  local copies, waits for them, and re-layouts: 2.51 us -> 0 us
    pallas_call x1 -> x2, Pallas kernels: 46.9 us -> 41.2 us  [the longest x1 40.4 us: on_device(): pl.pallas_call(kernel, out_shape=tuple((pltpu.VMEM(one.shape, one.dtype)...]
    unnamed x4 -> x0, local copies, waits for them, and re-layouts: 2.51 us -> none
where the time goes in v2:
time: 41.9 us; the launch traced here: 41.8 us
  Pallas kernels  41.2 us (98%)
  between operations  0.64 us (2%)
    pallas_call x1, Pallas kernels, on_device(): pl.pallas_call(kernel, out_shape=tuple((pltpu.VMEM(one.shape, one.dtype)...  40.4 us

profile of v2, /device:TPU:1, one launch (start us, length us, event | category | flops | bytes accessed | tf_op | source)
XLA Modules:
  0.0 41.8 jit_solution(11886877219399937511)
XLA Ops:
  0.6 40.4 %shard_map.50 = (bf16[8,16,16,128]{3,2,1,0:T(8,128)(2,1)S(1)}, f32[27,4,128]{2,1,0:T(4,128)S(1)}) custom-call(f32[27,4,128]{2,1,0:T(4,128)} %bitcast.2, bf16[8,16,16,128]{3,2,1,0:T(8,128)(2,1)} %in_hbm.1, bf16[8,16,16,128]{3,2,1,0:T(8,128)(2,1)} %cot_hbm.1), custom_call_target="tpu_custom_call" | custom-call | tf_op jit(solution)/shard_map/pallas_call | solution.py:483
  41.0 0.8 %shard_map.51 = (bf16[8,16,16,128]{3,2,1,0:T(8,128)(2,1)}, f32[27,4,128]{2,1,0:T(4,128)}) custom-call(bf16[8,16,16,128]{3,2,1,0:T(8,128)(2,1)S(1)} %get-tuple-element.6.dx_ref, f32[27,4,128]{2,1,0:T(4,128)S(1)} %get-tuple-element.7.wg_ref), custom_call_target="tpu_custom_call" | custom-call | tf_op jit(solution)/shard_map/pallas_call | solution.py:496

commit v3 on v2

v3 whole, which is shorter than its diff:
```python
import functools

import jax
import jax.numpy as jnp
from jax import lax
from jax.experimental import pallas as pl
from jax.experimental.pallas import tpu as pltpu
from jax.sharding import PartitionSpec as P

var_eps = 1e-05
norm_eps = 1e-06
clip_norm = 600.0
F32 = jnp.float32
BF16 = jnp.bfloat16
MESH = pl.DeviceIdType.MESH
AXES = ("gx", "gy", "gz")

NCORE, NZL, NYC, NXC, NZH = 2, 4, 4, 4, 2
NZR = NZL * NZH
CHUNKS = ((0, 8, 2, 0), (8, 8, 2, 2), (16, 11, 3, 4))
SLOTS = 7


def kernel(raw_hbm, in_hbm, cot_hbm, dx_ref, wg_ref, *scratch):
    (raw_ref, in_ref, shifted, face_out, edge_out, corner_out, face_in, edge_in, corner_in, up_out, up_in, in_t,
     part, recv_c, send_xy, recv_xy, recv_z, full, wz, w_all, w_cat, stats_w, stats_g,
     load_sem, sends, halo_recv, recvs, hello) = scratch
    taps, rows, chan = raw_ref.shape
    ex, ey, ez = in_ref.shape[:3]
    fan_count = float(rows * NCORE * NZL * NYC * taps)
    count = {"gx": NCORE * NZL, "gy": NYC, "gz": NXC * NZH}
    me = {axis: lax.axis_index(axis) for axis in AXES}
    core, zl = lax.rem(me["gx"], NCORE), lax.div(me["gx"], NCORE)
    my = me["gy"]
    mx, zh = lax.rem(me["gz"], NXC), lax.div(me["gz"], NXC)
    mz = zh * NZL + zl

    def spot(c=None, x=None, y=None, z=None):
        c = core if c is None else c
        x = mx if x is None else x
        y = my if y is None else y
        z = mz if z is None else z
        return {"gx": lax.rem(z, NZL) * NCORE + c, "gy": y, "gz": lax.div(z, NZL) * NXC + x}

    partner = spot(c=1 - core)
    x_line = [lax.rem(mx + k, NXC) for k in range(1, NXC)]
    y_line = [lax.rem(my + k, NYC) for k in range(1, NYC)]

    def xy_peer(k):
        flat = lax.rem(my * NXC + mx + k, NXC * NYC)
        return lax.rem(flat, NXC), lax.div(flat, NXC)

    flat_g = (my * NXC + mx) * NCORE + core

    def stat_peer(k):
        flat = lax.rem(flat_g + k, 32)
        where = lax.div(flat, NCORE)
        return spot(c=lax.rem(flat, NCORE), x=lax.rem(where, NXC), y=lax.div(where, NXC))

    def z_peer(k):
        return spot(z=lax.rem(mz + k, NZR))

    def remote(src, dst, send_sem, recv_sem, where):
        return pltpu.make_async_remote_copy(
            src_ref=src, dst_ref=dst, send_sem=send_sem, recv_sem=recv_sem,
            device_id=where, device_id_type=MESH,
        )

    def group(copies, wholes, send_sem, recv_sem):
        for src, dst, where in copies:
            remote(src, dst, send_sem, recv_sem, where).start()
        return remote(wholes, wholes, send_sem, recv_sem, partner)

    body = pl.ds(1, ey)
    load_cot = pltpu.make_async_copy(cot_hbm, shifted.at[1, pl.ds(1, ex), body], load_sem.at[0])
    load_in = pltpu.make_async_copy(in_hbm, in_ref, load_sem.at[1])
    load_raw = pltpu.make_async_copy(raw_hbm, raw_ref, load_sem.at[2])
    load_cot.start()
    load_in.start()
    load_raw.start()

    low = {axis: me[axis] == 0 for axis in AXES}
    high = {axis: me[axis] == count[axis] - 1 for axis in AXES}
    plane_offs = [(a, b, 0) for a in (1, -1, 0) for b in (0, 1, -1) if (a, b) != (0, 0)]
    down_offs = [(a, b, -1) for a in (0, 1, -1) for b in (0, 1, -1)]
    up_offs = [(-a, -b, 1) for a, b, _ in down_offs]

    def neighbour(off):
        return {axis: lax.rem(me[axis] + count[axis] + o, count[axis]) for axis, o in zip(AXES, off)}

    def exists(off):
        ok = None
        for axis, o in zip(AXES, off):
            if o != 0:
                one = me[axis] < count[axis] - 1 if o > 0 else me[axis] > 0
                ok = one if ok is None else jnp.logical_and(ok, one)
        return ok

    barrier = pltpu.get_barrier_semaphore()
    for off in up_offs + plane_offs:

        @pl.when(exists(off))
        def _():
            pl.semaphore_signal(barrier, inc=1, device_id=neighbour(off), device_id_type=MESH)

    near_z = [spot(z=lax.rem(mz + k, NZR)) for k in (1, 2, NZR - 2, NZR - 1)]
    lines = [spot(c=c, x=x) for x in x_line for c in range(NCORE)]
    lines += [spot(c=c, y=y) for y in y_line for c in range(NCORE)]
    for where in near_z + lines:
        pl.semaphore_signal(barrier, inc=1, device_id=where, device_id_type=MESH)

    def sides(axis):
        return (me[axis] > 0).astype(jnp.int32), (me[axis] < count[axis] - 1).astype(jnp.int32)

    around = (1 + sum(sides("gx"))) * (1 + sum(sides("gy")))
    greeted = around - 1 + around * sides("gz")[0] + len(near_z) + len(lines)

    tile = jnp.zeros((16, chan), BF16)
    for end, at_end in enumerate((low, high)):

        @pl.when(at_end["gx"])
        def _():
            shifted[1, (ex + 1) * end] = jnp.zeros((ey + 2, ez, chan), BF16)
            for side in range(2):
                face_in[side, (ex + 1) * end] = tile
                for b in range(2):
                    corner_in[side, b, end] = jnp.zeros((2, chan), BF16)

        @pl.when(at_end["gy"])
        def _():
            shifted[1, :, (ey + 1) * end] = jnp.zeros((ex + 2, ez, chan), BF16)
            for side in range(2):
                edge_in[side, end] = jnp.zeros((ex, chan), BF16)
                for a in range(2):
                    corner_in[side, end, a] = jnp.zeros((2, chan), BF16)

        @pl.when(at_end["gz"])
        def _():
            face_in[end] = jnp.zeros((ex + 2, ey, chan), BF16)
            edge_in[end] = jnp.zeros((2, ex, chan), BF16)
            corner_in[end] = jnp.zeros((2, 2, 2, chan), BF16)
            if end:
                up_in[...] = jnp.zeros((ex, ey, chan), BF16)

    w_all[taps] = jnp.zeros((8, 16, chan), BF16)
    for y in range(NYC):
        send_xy[y, taps] = tile
    with jax.named_scope("w_cot"):
        load_cot.wait()

    def make_faces(f, z):
        firsts, lasts = [], []
        for x in range(ex):
            face = shifted[1, x + 1, 1:ey + 1].astype(F32)[:, z, :]
            face_out[f, x] = face.astype(BF16)
            firsts.append(face[0:1])
            lasts.append(face[ey - 1:ey])
        for b, edge in enumerate((firsts, lasts)):
            edge_out[f, b] = jnp.concatenate(edge, axis=0).astype(BF16)
            for a, x in enumerate((0, ex - 1)):
                corner_out[f, b, a] = jnp.concatenate([edge[x], edge[x]], axis=0).astype(BF16)

    make_faces(0, 0)
    load_in.wait()
    for x in range(ex):
        up_out[x] = in_ref[x].astype(F32)[:, 0, :].astype(BF16)
    with jax.named_scope("w_barrier"):
        pl.semaphore_wait(barrier, greeted)

    def halo_copy(n, off, send=None):
        a, b, c = off
        near = {1: (ex, ey), -1: (1, 1)}
        if c == 0:
            xs = pl.ds(1, ex) if a == 0 else near[a][0]
            ys = body if b == 0 else near[b][1]
            xd = pl.ds(1, ex) if a == 0 else (0 if a > 0 else ex + 1)
            yd = body if b == 0 else (0 if b > 0 else ey + 1)
            src, dst = shifted.at[1, xs, ys], shifted.at[1, xd, yd]
        else:
            f, side = (1, 0) if c > 0 else (0, 1)
            if b == 0:
                xs = pl.ds(0, ex) if a == 0 else (ex - 1 if a > 0 else 0)
                xd = pl.ds(1, ex) if a == 0 else (0 if a > 0 else ex + 1)
                src, dst = face_out.at[f, xs], face_in.at[side, xd]
            else:
                end, ys = (1, 0) if b > 0 else (0, 1)
                src = edge_out.at[f, end] if a == 0 else corner_out.at[f, end, 1 if a > 0 else 0]
                dst = edge_in.at[side, ys] if a == 0 else corner_in.at[side, ys, 0 if a > 0 else 1]
        return remote(src, dst, sends.at[n if send is None else send], halo_recv.at[n], neighbour(off))

    down = [(off, halo_copy(n, off)) for n, off in enumerate(down_offs)]
    down_in = [((0, 0, -1), remote(up_out, up_in, sends.at[17], halo_recv.at[17], neighbour((0, 0, -1))))]
    plane = [(off, halo_copy(9 + n, off)) for n, off in enumerate(plane_offs)]
    up = [(off, halo_copy(18 + n, off, n)) for n, off in enumerate(up_offs)]

    def halo_do(halos, act, flip):
        for off, copy in halos:

            @pl.when(exists(tuple(-o for o in off) if flip else off))
            def _():
                act(copy)

    def halo_start(halos):
        halo_do(halos, lambda copy: copy.start(), False)

    def halo_sent(halos):
        halo_do(halos, lambda copy: copy.wait_send(), False)

    def halo_wait(halos):
        halo_do(halos, lambda copy: copy.wait_recv(), True)

    halo_start(plane)
    halo_start(down_in)
    halo_start(down)
    for where in near_z + [spot(x=x) for x in x_line]:
        pl.semaphore_signal(hello, inc=1, device_id=where, device_id_type=MESH)

    row_i = lax.broadcasted_iota(jnp.int32, (chan, chan), 0)
    col_i = lax.broadcasted_iota(jnp.int32, (chan, chan), 1)

    def natural(i):
        return (i // 4 % 4) * 32 + (i // 64) * 16 + (i // 16 % 4) * 4 + i % 4

    to_mine = jnp.where(col_i == natural(row_i), 1.0, 0.0).astype(BF16)
    to_natural = jnp.where(row_i == natural(col_i), 1.0, 0.0).astype(BF16)

    def transpose_in(slot, x, block):
        in_t[slot, :, x * ey * ez:(x + 1) * ey * ez] = lax.dot_general(
            to_mine, block.reshape(ey * ez, chan), (((1,), (1,)), ((), ())), preferred_element_type=F32
        ).astype(BF16)

    for x in range(ex):
        transpose_in(0, x, in_ref[x])

    order = [t for c in (1, 2, 0) for t in range(c, taps, 3)]

    def per_output(value):
        return jnp.sum(jnp.sum(value, axis=0), axis=0, keepdims=True)

    load_raw.wait()
    raw = raw_ref[...]
    raw_sum = per_output(raw)
    slab = core * NYC + my
    stats_w[slab, zl] = jnp.concatenate([raw_sum, per_output(raw * raw)], axis=0)
    local_mean = raw_sum / float(rows * taps)
    for u, t in enumerate(order):
        wz[zl, u] = (raw_ref[t] - local_mean).astype(BF16)
    make_faces(1, ez - 1)
    with jax.named_scope("w_hello"):
        pl.semaphore_wait(hello, len(near_z) + len(x_line))
    w1_copies = []
    for k in range(1, NZL):
        where = spot(z=zh * NZL + lax.rem(zl + k, NZL))
        w1_copies.append((wz.at[zl], wz.at[zl], where))
    gather_z = group(w1_copies, wz.at[pl.ds(0, NZL - 1)], sends.at[18], recvs.at[9])
    stats_z = group(
        [(stats_w.at[slab, zl], stats_w.at[slab, zl], where) for _, _, where in w1_copies],
        stats_w.at[slab, pl.ds(0, NZL - 1)], sends.at[19], recvs.at[10],
    )

    def view(slot, t, start, planes):
        a, b = t // 9, (t // 3) % 3
        block = shifted[slot, pl.ds(start + 2 - a, planes), 2 - b:2 - b + ey]
        return block.reshape(planes * ey * ez, chan)

    half_rows = chan // NCORE
    kinds = {1: (0, 1), 2: (1, 1), 0: (0, 2)}

    def filter_chunk(n):
        first, done, _, _ = CHUNKS[n]
        u = first
        while u < first + done:
            both = [u]
            if u + 1 < first + done and order[u + 1] % 3 == order[u] % 3:
                both.append(u + 1)
            left, slot = kinds[order[u] % 3]
            views = [view(slot, order[v], 0, ex) for v in both]
            right = jnp.concatenate(views, axis=1) if len(views) > 1 else views[0]
            product = jnp.dot(in_t[left], right, preferred_element_type=F32)
            for j, v in enumerate(both):
                for c in range(NCORE):
                    part[c, v] = product[c * half_rows:(c + 1) * half_rows, j * chan:(j + 1) * chan]
            u += len(both)
        span = pl.ds(first, done)
        return group(
            [(part.at[1 - core, span], recv_c.at[span], partner)], recv_c.at[span], sends.at[9 + n], recvs.at[n]
        )

    def xy_chunk(n, copy):
        first, done, each, slot = CHUNKS[n]
        with jax.named_scope("w_core%d" % n):
            copy.wait_recv()
        for v in range(first, first + done):
            total = part[core, v] + recv_c[v]
            for y in range(NYC):
                send_xy[y, v] = total[y * 16:(y + 1) * 16].astype(BF16)
        copies = []
        for k in range(1, NXC * NYC):
            px, py = xy_peer(k)
            copies.append((
                send_xy.at[py, pl.ds(first + px * each, each)], recv_xy.at[k - 1, pl.ds(slot, each)],
                spot(x=px, y=py),
            ))
        return group(copies, recv_xy.at[:, pl.ds(slot, each)], sends.at[12 + n], recvs.at[3 + n])

    def z_chunk(n, copy):
        first, done, each, slot = CHUNKS[n]
        with jax.named_scope("w_xy%d" % n):
            copy.wait_recv()
        span = pl.ds(slot, each)
        total = send_xy[my, pl.ds(first + mx * each, each)].astype(F32)
        for k in range(1, NXC * NYC):
            total = total + recv_xy[k - 1, span].astype(F32)
        recv_z[mz, span] = total.astype(BF16)
        return group(
            [(recv_z.at[mz, span], recv_z.at[mz, span], z_peer(k)) for k in range(1, NZR)],
            recv_z.at[pl.ds(0, NZR - 1), span], sends.at[15 + n], recvs.at[6 + n],
        )

    def shift(slot, side, amount, edge):
        depth = lax.broadcasted_iota(jnp.int32, (ey, ez, chan), 1)
        for x in range(ex + 2):
            plane = shifted[1, x, 1:ey + 1].astype(F32)
            outer = face_in[side, x].astype(F32)[:, None, :]
            shifted[slot, x, 1:ey + 1] = jnp.where(depth == edge, outer, pltpu.roll(plane, amount, 1)).astype(BF16)
        depth = lax.broadcasted_iota(jnp.int32, (ex + 2, ez, chan), 1)
        for b in range(2):
            y = (ey + 1) * b
            plane = shifted[1, :, y].astype(F32)
            outer = jnp.concatenate([
                corner_in[side, b, 0].astype(F32)[0:1], edge_in[side, b].astype(F32),
                corner_in[side, b, 1].astype(F32)[0:1],
            ], axis=0)[:, None, :]
            shifted[slot, :, y] = jnp.where(depth == edge, outer, pltpu.roll(plane, amount, 1)).astype(BF16)

    with jax.named_scope("w_halo_xy"):
        halo_wait(plane)
    with jax.named_scope("w_halo_sent"):
        halo_sent(plane)
        halo_sent(down_in)
        halo_sent(down)
    core_0 = filter_chunk(0)
    with jax.named_scope("w_halo_in"):
        halo_wait(down_in)
    depth = lax.broadcasted_iota(jnp.int32, (ey, ez, chan), 1)
    for x in range(ex):
        outer = up_in[x].astype(F32)[:, None, :]
        moved = pltpu.roll(in_ref[x].astype(F32), ez - 1, 1)
        transpose_in(1, x, jnp.where(depth == ez - 1, outer, moved).astype(BF16))
    core_1 = filter_chunk(1)
    xy_0 = xy_chunk(0, core_0)
    with jax.named_scope("w_halo_z"):
        halo_wait(down)
    halo_start(up)
    shift(2, 1, ez - 1, ez - 1)
    core_2 = filter_chunk(2)
    xy_1 = xy_chunk(1, core_1)
    with jax.named_scope("w_gather_z"):
        gather_z.wait_recv()
        stats_z.wait_recv()
    for u in range(taps):
        w_all[u, slab] = wz[:, u].astype(F32).reshape(16, chan).astype(BF16)
    core_0.wait_send()
    core_1.wait_send()
    tap_span = pl.ds(0, taps)
    gather_y = group(
        [(w_all.at[tap_span, slab], w_all.at[tap_span, slab], spot(y=y)) for y in y_line],
        w_all.at[tap_span, pl.ds(0, NYC - 1)], sends.at[9], recvs.at[11],
    )
    stats_y = group(
        [(stats_w.at[slab], stats_w.at[slab], spot(y=y)) for y in y_line],
        stats_w.at[pl.ds(0, NYC - 1)], sends.at[10], recvs.at[12],
    )
    xy_2 = xy_chunk(2, core_2)
    z_0 = z_chunk(0, xy_0)
    z_1 = z_chunk(1, xy_1)
    with jax.named_scope("w_halo_up"):
        halo_wait(up)
        halo_sent(up)
    shift(0, 0, 1, 0)
    z_2 = z_chunk(2, xy_2)
    with jax.named_scope("w_gather_y"):
        gather_y.wait_recv()
        stats_y.wait_recv()
    core_2.wait_send()
    xy_0.wait_send()
    slabs = w_all.at[tap_span, pl.ds(core * NYC, NYC)]
    gather_c = group([(slabs, slabs, partner)], slabs, sends.at[11], recvs.at[13])
    mine = stats_w.at[pl.ds(core * NYC, NYC)]
    stats_c = group([(mine, mine, partner)], mine, sends.at[12], recvs.at[14])
    with jax.named_scope("w_z"):
        z_0.wait_recv()
        z_1.wait_recv()
        z_2.wait_recv()
    grad = recv_z[0].astype(F32)
    for k in range(1, NZR):
        grad = grad + recv_z[k].astype(F32)
    pivot = stats_w[slab, 0][0:1]
    gap = [jnp.broadcast_to((stats_w[slab, q][0:1] - pivot) / float(rows * taps), (rows, chan)) for q in range(NZL)]
    gap = jnp.concatenate(gap, axis=0)
    near = []
    for first, _, each, _ in CHUNKS:
        near += [w_all[first + mx * each + j, slab].astype(F32) for j in range(each)]
    cross = grad[0] * (near[0] + gap)
    for j in range(1, SLOTS):
        cross = cross + grad[j] * (near[j] + gap)
    stats_g[flat_g] = jnp.concatenate(
        [per_output(grad), jnp.sum(cross, axis=0, keepdims=True), per_output(grad * grad), jnp.zeros((1, chan), F32)],
        axis=0,
    )
    xy_1.wait_send()
    xy_2.wait_send()
    grad_sums = group(
        [(stats_g.at[flat_g], stats_g.at[flat_g], stat_peer(k)) for k in range(1, 32)],
        stats_g.at[pl.ds(0, 31)], sends.at[13], recvs.at[15],
    )
    for j in range(SLOTS):
        owned = grad[j, 0:rows]
        for q in range(1, NZL):
            owned = jnp.where(zl == q, grad[j, q * rows:(q + 1) * rows], owned)
        full[mx, j] = owned
    gather_x = group(
        [(full.at[mx], full.at[mx], spot(x=x)) for x in x_line],
        full.at[pl.ds(0, NXC - 1)], sends.at[14], recvs.at[16],
    )

    with jax.named_scope("w_gather_c"):
        gather_c.wait_recv()
        stats_c.wait_recv()
    sums = stats_w[0, 0]
    for k in range(1, 32):
        sums = sums + stats_w[k // NZL, k % NZL]
    mean_out = sums[0:1] / fan_count
    var_out = sums[1:2] / fan_count - mean_out * mean_out
    inv_std = lax.rsqrt(var_out + var_eps)
    offset = []
    for k in range(32):
        gap = stats_w[k // NZL, k % NZL][0:1] / float(rows * taps) - mean_out
        offset.append(jnp.broadcast_to(gap, (rows, chan)))
    offset = jnp.concatenate(offset, axis=0)
    for u in range(0, taps, 2):
        pair = range(u, min(u + 2, taps))
        right = []
        for v in pair:
            value = (w_all[v].reshape(chan, chan).astype(F32) + offset) * inv_std
            right.append(value.astype(BF16))
        right = jnp.concatenate(right, axis=1) if len(right) > 1 else right[0]
        w_cat[:, u * chan:(u + len(pair)) * chan] = jnp.dot(
            to_natural, right, preferred_element_type=F32
        ).astype(BF16)
    step = 2

    def dx_step(n, carry):
        start = n * step
        left = jnp.concatenate([view(2 - t % 3, t, start, step) for t in order], axis=1)
        product = lax.dot_general(left, w_cat[...], (((1,), (1,)), ((), ())), preferred_element_type=F32)
        dx_ref[pl.ds(start, step)] = product.astype(BF16).reshape(step, ey, ez, chan)
        return carry

    with jax.named_scope("dx"):
        lax.fori_loop(0, ex // step, dx_step, 0)

    with jax.named_scope("w_grad_sums"):
        grad_sums.wait_recv()
    with jax.named_scope("w_gather_x"):
        gather_x.wait_recv()
    sum_grad, sum_cross, sum_square = (jnp.zeros((1, chan), F32) for _ in range(3))
    for k in range(32):
        one = stats_g[k]
        about = stats_w[k % NCORE * NYC + k // (NXC * NCORE), 0][0:1] / float(rows * taps) - mean_out
        sum_grad = sum_grad + one[0:1]
        sum_cross = sum_cross + (one[1:2] + about * one[0:1])
        sum_square = sum_square + one[2:3]
    sum_cross = sum_cross * inv_std
    mean_grad = sum_grad / fan_count
    mean_cross = sum_cross / fan_count
    spread = sum_square - 2.0 * mean_grad * sum_grad - 2.0 * mean_cross * sum_cross
    spread = (
        spread
        + fan_count * mean_grad * mean_grad
        + fan_count * mean_cross * mean_cross * var_out / (var_out + var_eps)
    )
    square_sum = jnp.sum(inv_std * inv_std * spread, axis=1, keepdims=True)
    scale = jnp.minimum(1.0, clip_norm * lax.rsqrt(square_sum + norm_eps))
    factor = inv_std * scale
    for first, done, each, slot in CHUNKS:
        for v in range(done):
            t = order[first + v]
            std = (raw_ref[t] - mean_out) * inv_std
            wg_ref[t] = factor * (full[v // each, slot + v % each] - mean_grad - std * mean_cross)

    with jax.named_scope("w_sends"):
        for copy in (gather_z, stats_z, gather_y, stats_y, gather_c, stats_c, z_0, z_1, z_2, grad_sums, gather_x):
            copy.wait_send()


def write_out(dx_ref, wg_ref, dx_hbm, wg_hbm, sem):
    copies = [pltpu.make_async_copy(dx_ref, dx_hbm, sem.at[0]), pltpu.make_async_copy(wg_ref, wg_hbm, sem.at[1])]
    for copy in copies:
        copy.start()
    for copy in copies:
        copy.wait()


def on_device(raw_weight, inputs, cotangent):
    rows, taps, chan = raw_weight.shape
    ex, ey, ez = inputs.shape[:3]
    dma = pltpu.SemaphoreType.DMA

    scratch = [
        pltpu.VMEM((taps, rows, chan), F32),
        pltpu.VMEM(inputs.shape, BF16),
        pltpu.VMEM((3, ex + 2, ey + 2, ez, chan), BF16),
        pltpu.VMEM((2, ex, ey, chan), BF16),
        pltpu.VMEM((2, 2, ex, chan), BF16),
        pltpu.VMEM((2, 2, 2, 2, chan), BF16),
        pltpu.VMEM((2, ex + 2, ey, chan), BF16),
        pltpu.VMEM((2, 2, ex, chan), BF16),
        pltpu.VMEM((2, 2, 2, 2, chan), BF16),
        pltpu.VMEM((ex, ey, chan), BF16),
        pltpu.VMEM((ex, ey, chan), BF16),
        pltpu.VMEM((2, chan, ex * ey * ez), BF16),
        pltpu.VMEM((NCORE, taps, chan // NCORE, chan), F32),
        pltpu.VMEM((taps, chan // NCORE, chan), F32),
        pltpu.VMEM((NYC, taps + 1, 16, chan), BF16),
        pltpu.VMEM((NXC * NYC - 1, SLOTS, 16, chan), BF16),
        pltpu.VMEM((NZR, SLOTS, 16, chan), BF16),
        pltpu.VMEM((NXC, SLOTS, rows, chan), F32),
        pltpu.VMEM((NZL, taps, rows, chan), BF16),
        pltpu.VMEM((taps + 1, 8, 16, chan), BF16),
        pltpu.VMEM((chan, taps * chan), BF16),
        pltpu.VMEM((8, NZL, 2, chan), F32),
        pltpu.VMEM((32, 4, chan), F32),
        dma((3,)), dma((20,)), dma((27,)), dma((17,)), pltpu.SemaphoreType.REGULAR,
    ]
    vmem = pl.BlockSpec(memory_space=pltpu.VMEM)
    anywhere = pl.BlockSpec(memory_space=pl.ANY)
    shapes = (
        jax.ShapeDtypeStruct(cotangent.shape, BF16),
        jax.ShapeDtypeStruct((taps, rows, chan), F32),
    )
    results = pl.pallas_call(
        kernel,
        out_shape=tuple(pltpu.VMEM(one.shape, one.dtype) for one in shapes),
        in_specs=[anywhere] * 3,
        out_specs=(vmem, vmem),
        scratch_shapes=scratch,
        compiler_params=pltpu.CompilerParams(
            collective_id=0, has_side_effects=True, vmem_limit_bytes=32 * 1024 * 1024
        ),
    )(*(
        pltpu.with_memory_space_constraint(one, pltpu.HBM)
        for one in (jnp.transpose(raw_weight, (1, 0, 2)), inputs, cotangent)
    ))
    input_grad, weight_grad = pl.pallas_call(
        write_out,
        out_shape=shapes,
        in_specs=[vmem, vmem],
        out_specs=(anywhere, anywhere),
        scratch_shapes=[dma((2,))],
    )(*(pltpu.with_memory_space_constraint(one, pltpu.VMEM) for one in results))
    return input_grad, jnp.transpose(weight_grad, (1, 0, 2))


def solution(mesh):
    in_specs = (P(("gx", "gy"), None, None), P("gx", "gy", "gz", None), P("gx", "gy", "gz", None))
    out_specs = (P("gx", "gy", "gz", None), P(("gx", "gy"), None, None))
    return jax.shard_map(
        on_device, mesh=mesh, in_specs=in_specs, out_specs=out_specs, check_vma=False
    )
```

time: 41.9 us -> 41.6 us (level)
  no operation moved by 1% of the time
where the time goes in v3:
time: 41.6 us; the launch traced here: 41.5 us
  Pallas kernels  40.8 us (98%)
  between operations  0.64 us (2%)
    pallas_call x1, Pallas kernels, on_device(): pl.pallas_call(kernel, out_shape=tuple((pltpu.VMEM(one.shape, one.dtype)...  40 us

profile of v3, /device:TPU:1, one launch (start us, length us, event | category | flops | bytes accessed | tf_op | source)
XLA Modules:
  0.0 41.5 jit_solution(4345074683800557893)
XLA Ops:
  0.6 40.0 %shard_map.50 = (bf16[8,16,16,128]{3,2,1,0:T(8,128)(2,1)S(1)}, f32[27,4,128]{2,1,0:T(4,128)S(1)}) custom-call(f32[27,4,128]{2,1,0:T(4,128)} %bitcast.2, bf16[8,16,16,128]{3,2,1,0:T(8,128)(2,1)} %in_hbm.1, bf16[8,16,16,128]{3,2,1,0:T(8,128)(2,1)} %cot_hbm.1), custom_call_target="tpu_custom_call" | custom-call | tf_op jit(solution)/shard_map/pallas_call | solution.py:542
  40.7 0.8 %shard_map.51 = (bf16[8,16,16,128]{3,2,1,0:T(8,128)(2,1)}, f32[27,4,128]{2,1,0:T(4,128)}) custom-call(bf16[8,16,16,128]{3,2,1,0:T(8,128)(2,1)S(1)} %get-tuple-element.6.dx_ref, f32[27,4,128]{2,1,0:T(4,128)S(1)} %get-tuple-element.7.wg_ref), custom_call_target="tpu_custom_call" | custom-call | tf_op jit(solution)/shard_map/pallas_call | solution.py:555

commit v4 on v3

--- a/solution.py
+++ b/solution.py
@@ -22,7 +22,7 @@
 
 
 def kernel(raw_hbm, in_hbm, cot_hbm, dx_ref, wg_ref, *scratch):
-    (raw_ref, in_ref, shifted, face_out, edge_out, corner_out, face_in, edge_in, corner_in, up_out, up_in, in_t,
+    (raw_ref, in_ref, shifted, face_out, edge_out, corner_out, face_in, edge_in, corner_in, in_out, in_in, in_t,
      part, recv_c, send_xy, recv_xy, recv_z, full, wz, w_all, w_cat, stats_w, stats_g,
      load_sem, sends, halo_recv, recvs, hello) = scratch
     taps, rows, chan = raw_ref.shape
@@ -97,7 +97,7 @@
         return ok
 
     barrier = pltpu.get_barrier_semaphore()
-    for off in up_offs + plane_offs:
+    for off in [(0, 0, 1), (0, 0, -1)] + plane_offs:
 
         @pl.when(exists(off))
         def _():
@@ -113,7 +113,7 @@
         return (me[axis] > 0).astype(jnp.int32), (me[axis] < count[axis] - 1).astype(jnp.int32)
 
     around = (1 + sum(sides("gx"))) * (1 + sum(sides("gy")))
-    greeted = around - 1 + around * sides("gz")[0] + len(near_z) + len(lines)
+    greeted = around - 1 + sum(sides("gz")) + len(near_z) + len(lines)
 
     tile = jnp.zeros((16, chan), BF16)
     for end, at_end in enumerate((low, high)):
@@ -139,8 +139,7 @@
             face_in[end] = jnp.zeros((ex + 2, ey, chan), BF16)
             edge_in[end] = jnp.zeros((2, ex, chan), BF16)
             corner_in[end] = jnp.zeros((2, 2, 2, chan), BF16)
-            if end:
-                up_in[...] = jnp.zeros((ex, ey, chan), BF16)
+            in_in[end] = jnp.zeros((ex, ey, chan), BF16)
 
     w_all[taps] = jnp.zeros((8, 16, chan), BF16)
     for y in range(NYC):
@@ -160,14 +159,15 @@
             for a, x in enumerate((0, ex - 1)):
                 corner_out[f, b, a] = jnp.concatenate([edge[x], edge[x]], axis=0).astype(BF16)
 
-    make_faces(0, 0)
     load_in.wait()
     for x in range(ex):
-        up_out[x] = in_ref[x].astype(F32)[:, 0, :].astype(BF16)
+        block = in_ref[x].astype(F32)
+        in_out[0, x] = block[:, 0, :].astype(BF16)
+        in_out[1, x] = block[:, ez - 1, :].astype(BF16)
     with jax.named_scope("w_barrier"):
         pl.semaphore_wait(barrier, greeted)
 
-    def halo_copy(n, off, send=None):
+    def halo_copy(n, off, send):
         a, b, c = off
         near = {1: (ex, ey), -1: (1, 1)}
         if c == 0:
@@ -186,12 +186,14 @@
                 end, ys = (1, 0) if b > 0 else (0, 1)
                 src = edge_out.at[f, end] if a == 0 else corner_out.at[f, end, 1 if a > 0 else 0]
                 dst = edge_in.at[side, ys] if a == 0 else corner_in.at[side, ys, 0 if a > 0 else 1]
-        return remote(src, dst, sends.at[n if send is None else send], halo_recv.at[n], neighbour(off))
-
-    down = [(off, halo_copy(n, off)) for n, off in enumerate(down_offs)]
-    down_in = [((0, 0, -1), remote(up_out, up_in, sends.at[17], halo_recv.at[17], neighbour((0, 0, -1))))]
-    plane = [(off, halo_copy(9 + n, off)) for n, off in enumerate(plane_offs)]
-    up = [(off, halo_copy(18 + n, off, n)) for n, off in enumerate(up_offs)]
+        return remote(src, dst, sends.at[send], halo_recv.at[n], neighbour(off))
+
+    plane = [(off, halo_copy(n, off, n)) for n, off in enumerate(plane_offs)]
+    in_lo, in_hi = (
+        [((0, 0, c), remote(in_out.at[f], in_in.at[1 - f], sends.at[8 + f], halo_recv.at[8 + f], neighbour((0, 0, c))))]
+        for f, c in ((1, 1), (0, -1))
+    )
+    along = [(off, halo_copy(10 + n, off, n)) for n, off in enumerate(down_offs + up_offs)]
 
     def halo_do(halos, act, flip):
         for off, copy in halos:
@@ -210,8 +212,8 @@
         halo_do(halos, lambda copy: copy.wait_recv(), True)
 
     halo_start(plane)
-    halo_start(down_in)
-    halo_start(down)
+    halo_start(in_hi)
+    halo_start(in_lo)
     for where in near_z + [spot(x=x) for x in x_line]:
         pl.semaphore_signal(hello, inc=1, device_id=where, device_id_type=MESH)
 
@@ -245,6 +247,7 @@
     local_mean = raw_sum / float(rows * taps)
     for u, t in enumerate(order):
         wz[zl, u] = (raw_ref[t] - local_mean).astype(BF16)
+    make_faces(0, 0)
     make_faces(1, ez - 1)
     with jax.named_scope("w_hello"):
         pl.semaphore_wait(hello, len(near_z) + len(x_line))
@@ -252,10 +255,10 @@
     for k in range(1, NZL):
         where = spot(z=zh * NZL + lax.rem(zl + k, NZL))
         w1_copies.append((wz.at[zl], wz.at[zl], where))
-    gather_z = group(w1_copies, wz.at[pl.ds(0, NZL - 1)], sends.at[18], recvs.at[9])
+    gather_z = group(w1_copies, wz.at[pl.ds(0, NZL - 1)], sends.at[27], recvs.at[9])
     stats_z = group(
         [(stats_w.at[slab, zl], stats_w.at[slab, zl], where) for _, _, where in w1_copies],
-        stats_w.at[slab, pl.ds(0, NZL - 1)], sends.at[19], recvs.at[10],
+        stats_w.at[slab, pl.ds(0, NZL - 1)], sends.at[28], recvs.at[10],
     )
 
     def view(slot, t, start, planes):
@@ -264,7 +267,7 @@
         return block.reshape(planes * ey * ez, chan)
 
     half_rows = chan // NCORE
-    kinds = {1: (0, 1), 2: (1, 1), 0: (0, 2)}
+    kinds = {1: 0, 2: 1, 0: 2}
 
     def filter_chunk(n):
         first, done, _, _ = CHUNKS[n]
@@ -273,17 +276,16 @@
             both = [u]
             if u + 1 < first + done and order[u + 1] % 3 == order[u] % 3:
                 both.append(u + 1)
-            left, slot = kinds[order[u] % 3]
-            views = [view(slot, order[v], 0, ex) for v in both]
+            views = [view(1, order[v], 0, ex) for v in both]
             right = jnp.concatenate(views, axis=1) if len(views) > 1 else views[0]
-            product = jnp.dot(in_t[left], right, preferred_element_type=F32)
+            product = jnp.dot(in_t[kinds[order[u] % 3]], right, preferred_element_type=F32)
             for j, v in enumerate(both):
                 for c in range(NCORE):
                     part[c, v] = product[c * half_rows:(c + 1) * half_rows, j * chan:(j + 1) * chan]
             u += len(both)
         span = pl.ds(first, done)
         return group(
-            [(part.at[1 - core, span], recv_c.at[span], partner)], recv_c.at[span], sends.at[9 + n], recvs.at[n]
+            [(part.at[1 - core, span], recv_c.at[span], partner)], recv_c.at[span], sends.at[18 + n], recvs.at[n]
         )
 
     def xy_chunk(n, copy):
@@ -301,7 +303,7 @@
                 send_xy.at[py, pl.ds(first + px * each, each)], recv_xy.at[k - 1, pl.ds(slot, each)],
                 spot(x=px, y=py),
             ))
-        return group(copies, recv_xy.at[:, pl.ds(slot, each)], sends.at[12 + n], recvs.at[3 + n])
+        return group(copies, recv_xy.at[:, pl.ds(slot, each)], sends.at[21 + n], recvs.at[3 + n])
 
     def z_chunk(n, copy):
         first, done, each, slot = CHUNKS[n]
@@ -314,7 +316,7 @@
         recv_z[mz, span] = total.astype(BF16)
         return group(
             [(recv_z.at[mz, span], recv_z.at[mz, span], z_peer(k)) for k in range(1, NZR)],
-            recv_z.at[pl.ds(0, NZR - 1), span], sends.at[15 + n], recvs.at[6 + n],
+            recv_z.at[pl.ds(0, NZR - 1), span], sends.at[24 + n], recvs.at[6 + n],
         )
 
     def shift(slot, side, amount, edge):
@@ -335,26 +337,30 @@
 
     with jax.named_scope("w_halo_xy"):
         halo_wait(plane)
-    with jax.named_scope("w_halo_sent"):
-        halo_sent(plane)
-        halo_sent(down_in)
-        halo_sent(down)
     core_0 = filter_chunk(0)
-    with jax.named_scope("w_halo_in"):
-        halo_wait(down_in)
-    depth = lax.broadcasted_iota(jnp.int32, (ey, ez, chan), 1)
-    for x in range(ex):
-        outer = up_in[x].astype(F32)[:, None, :]
-        moved = pltpu.roll(in_ref[x].astype(F32), ez - 1, 1)
-        transpose_in(1, x, jnp.where(depth == ez - 1, outer, moved).astype(BF16))
+
+    def move_in(kind, side, amount, edge):
+        depth = lax.broadcasted_iota(jnp.int32, (ey, ez, chan), 1)
+        for x in range(ex):
+            outer = in_in[side, x].astype(F32)[:, None, :]
+            moved = pltpu.roll(in_ref[x].astype(F32), amount, 1)
+            transpose_in(kind, x, jnp.where(depth == edge, outer, moved).astype(BF16))
+
+    with jax.named_scope("w_halo_hi"):
+        halo_wait(in_hi)
+    move_in(1, 1, ez - 1, ez - 1)
     core_1 = filter_chunk(1)
     xy_0 = xy_chunk(0, core_0)
-    with jax.named_scope("w_halo_z"):
-        halo_wait(down)
-    halo_start(up)
-    shift(2, 1, ez - 1, ez - 1)
+    with jax.named_scope("w_halo_lo"):
+        halo_wait(in_lo)
+    halo_sent(plane)
+    halo_sent(in_hi)
+    halo_sent(in_lo)
+    halo_start(along)
+    move_in(2, 0, 1, 0)
     core_2 = filter_chunk(2)
     xy_1 = xy_chunk(1, core_1)
+    xy_2 = xy_chunk(2, core_2)
     with jax.named_scope("w_gather_z"):
         gather_z.wait_recv()
         stats_z.wait_recv()
@@ -365,29 +371,29 @@
     tap_span = pl.ds(0, taps)
     gather_y = group(
         [(w_all.at[tap_span, slab], w_all.at[tap_span, slab], spot(y=y)) for y in y_line],
-        w_all.at[tap_span, pl.ds(0, NYC - 1)], sends.at[9], recvs.at[11],
+        w_all.at[tap_span, pl.ds(0, NYC - 1)], sends.at[18], recvs.at[11],
     )
     stats_y = group(
         [(stats_w.at[slab], stats_w.at[slab], spot(y=y)) for y in y_line],
-        stats_w.at[pl.ds(0, NYC - 1)], sends.at[10], recvs.at[12],
-    )
-    xy_2 = xy_chunk(2, core_2)
+        stats_w.at[pl.ds(0, NYC - 1)], sends.at[19], recvs.at[12],
+    )
     z_0 = z_chunk(0, xy_0)
     z_1 = z_chunk(1, xy_1)
-    with jax.named_scope("w_halo_up"):
-        halo_wait(up)
-        halo_sent(up)
+    z_2 = z_chunk(2, xy_2)
+    with jax.named_scope("w_halo_along"):
+        halo_wait(along)
+        halo_sent(along)
+    shift(2, 1, ez - 1, ez - 1)
     shift(0, 0, 1, 0)
-    z_2 = z_chunk(2, xy_2)
     with jax.named_scope("w_gather_y"):
         gather_y.wait_recv()
         stats_y.wait_recv()
     core_2.wait_send()
     xy_0.wait_send()
     slabs = w_all.at[tap_span, pl.ds(core * NYC, NYC)]
-    gather_c = group([(slabs, slabs, partner)], slabs, sends.at[11], recvs.at[13])
+    gather_c = group([(slabs, slabs, partner)], slabs, sends.at[20], recvs.at[13])
     mine = stats_w.at[pl.ds(core * NYC, NYC)]
-    stats_c = group([(mine, mine, partner)], mine, sends.at[12], recvs.at[14])
+    stats_c = group([(mine, mine, partner)], mine, sends.at[21], recvs.at[14])
     with jax.named_scope("w_z"):
         z_0.wait_recv()
         z_1.wait_recv()
@@ -412,7 +418,7 @@
     xy_2.wait_send()
     grad_sums = group(
         [(stats_g.at[flat_g], stats_g.at[flat_g], stat_peer(k)) for k in range(1, 32)],
-        stats_g.at[pl.ds(0, 31)], sends.at[13], recvs.at[15],
+        stats_g.at[pl.ds(0, 31)], sends.at[22], recvs.at[15],
     )
     for j in range(SLOTS):
         owned = grad[j, 0:rows]
@@ -421,7 +427,7 @@
         full[mx, j] = owned
     gather_x = group(
         [(full.at[mx], full.at[mx], spot(x=x)) for x in x_line],
-        full.at[pl.ds(0, NXC - 1)], sends.at[14], recvs.at[16],
+        full.at[pl.ds(0, NXC - 1)], sends.at[23], recvs.at[16],
     )
 
     with jax.named_scope("w_gather_c"):
@@ -517,9 +523,9 @@
         pltpu.VMEM((2, ex + 2, ey, chan), BF16),
         pltpu.VMEM((2, 2, ex, chan), BF16),
         pltpu.VMEM((2, 2, 2, 2, chan), BF16),
-        pltpu.VMEM((ex, ey, chan), BF16),
-        pltpu.VMEM((ex, ey, chan), BF16),
-        pltpu.VMEM((2, chan, ex * ey * ez), BF16),
+        pltpu.VMEM((2, ex, ey, chan), BF16),
+        pltpu.VMEM((2, ex, ey, chan), BF16),
+        pltpu.VMEM((3, chan, ex * ey * ez), BF16),
         pltpu.VMEM((NCORE, taps, chan // NCORE, chan), F32),
         pltpu.VMEM((taps, chan // NCORE, chan), F32),
         pltpu.VMEM((NYC, taps + 1, 16, chan), BF16),
@@ -531,7 +537,7 @@
         pltpu.VMEM((chan, taps * chan), BF16),
         pltpu.VMEM((8, NZL, 2, chan), F32),
         pltpu.VMEM((32, 4, chan), F32),
-        dma((3,)), dma((20,)), dma((27,)), dma((17,)), pltpu.SemaphoreType.REGULAR,
+        dma((3,)), dma((29,)), dma((28,)), dma((17,)), pltpu.SemaphoreType.REGULAR,
     ]
     vmem = pl.BlockSpec(memory_space=pltpu.VMEM)
     anywhere = pl.BlockSpec(memory_space=pl.ANY)

time: 41.6 us -> 38.9 us (0.935)
  Pallas kernels: 40.8 us -> 38.2 us
    pallas_call x1, Pallas kernels: 40 us -> 37.3 us  [on_device(): pl.pallas_call(kernel, out_shape=tuple((pltpu.VMEM(one.shape, one.dtype)...]
where the time goes in v4:
time: 38.9 us; the launch traced here: 38.8 us
  Pallas kernels  38.2 us (98%)
  between operations  0.64 us (2%)
    pallas_call x1, Pallas kernels, on_device(): pl.pallas_call(kernel, out_shape=tuple((pltpu.VMEM(one.shape, one.dtype)...  37.3 us
    pallas_call x1, Pallas kernels, on_device(): pl.pallas_call(write_out, out_shape=shapes, in_specs=[vmem, vmem], out_sp...  0.81 us

profile of v4, /device:TPU:1, one launch (start us, length us, event | category | flops | bytes accessed | tf_op | source)
XLA Modules:
  0.0 38.8 jit_solution(18202659541367166535)
XLA Ops:
  0.6 37.3 %shard_map.50 = (bf16[8,16,16,128]{3,2,1,0:T(8,128)(2,1)S(1)}, f32[27,4,128]{2,1,0:T(4,128)S(1)}) custom-call(f32[27,4,128]{2,1,0:T(4,128)} %bitcast.2, bf16[8,16,16,128]{3,2,1,0:T(8,128)(2,1)} %in_hbm.1, bf16[8,16,16,128]{3,2,1,0:T(8,128)(2,1)} %cot_hbm.1), custom_call_target="tpu_custom_call" | custom-call | tf_op jit(solution)/shard_map/pallas_call | solution.py:548
  38.0 0.8 %shard_map.51 = (bf16[8,16,16,128]{3,2,1,0:T(8,128)(2,1)}, f32[27,4,128]{2,1,0:T(4,128)}) custom-call(bf16[8,16,16,128]{3,2,1,0:T(8,128)(2,1)S(1)} %get-tuple-element.6.dx_ref, f32[27,4,128]{2,1,0:T(4,128)S(1)} %get-tuple-element.7.wg_ref), custom_call_target="tpu_custom_call" | custom-call | tf_op jit(solution)/shard_map/pallas_call | solution.py:561

commit v5 on v4

v5 whole, which is shorter than its diff:
```python
import functools

import jax
import jax.numpy as jnp
from jax import lax
from jax.experimental import pallas as pl
from jax.experimental.pallas import tpu as pltpu
from jax.sharding import PartitionSpec as P

var_eps = 1e-05
norm_eps = 1e-06
clip_norm = 600.0
F32 = jnp.float32
BF16 = jnp.bfloat16
MESH = pl.DeviceIdType.MESH
AXES = ("gx", "gy", "gz")

NCORE, NZL, NYC, NXC, NZH = 2, 4, 4, 4, 2
NZR = NZL * NZH
CHUNKS = ((0, 8, 2, 0), (8, 8, 2, 2), (16, 11, 3, 4))
SLOTS = 7
W_SPLIT = 9


def kernel(raw_hbm, in_hbm, cot_hbm, dx_ref, wg_ref, *scratch):
    (raw_ref, in_ref, shifted, halo_x, halo_y, along_out, along_in, in_out, in_in, in_t, edge_y, edge_t, rim, rim_view,
     part, recv_c, send_xy, recv_xy, recv_z, full, wz, w_all, w_cat, dx_acc, stats_w, stats_g,
     load_sem, sends, halo_recv, recvs, hello) = scratch
    taps, rows, chan = raw_ref.shape
    ex, ey, ez = in_ref.shape[:3]
    fan_count = float(rows * NCORE * NZL * NYC * taps)
    count = {"gx": NCORE * NZL, "gy": NYC, "gz": NXC * NZH}
    me = {axis: lax.axis_index(axis) for axis in AXES}
    core, zl = lax.rem(me["gx"], NCORE), lax.div(me["gx"], NCORE)
    my = me["gy"]
    mx, zh = lax.rem(me["gz"], NXC), lax.div(me["gz"], NXC)
    mz = zh * NZL + zl

    def spot(c=None, x=None, y=None, z=None):
        c = core if c is None else c
        x = mx if x is None else x
        y = my if y is None else y
        z = mz if z is None else z
        return {"gx": lax.rem(z, NZL) * NCORE + c, "gy": y, "gz": lax.div(z, NZL) * NXC + x}

    partner = spot(c=1 - core)
    x_line = [lax.rem(mx + k, NXC) for k in range(1, NXC)]
    y_line = [lax.rem(my + k, NYC) for k in range(1, NYC)]

    def xy_peer(k):
        flat = lax.rem(my * NXC + mx + k, NXC * NYC)
        return lax.rem(flat, NXC), lax.div(flat, NXC)

    flat_g = (my * NXC + mx) * NCORE + core

    def stat_peer(k):
        flat = lax.rem(flat_g + k, 32)
        where = lax.div(flat, NCORE)
        return spot(c=lax.rem(flat, NCORE), x=lax.rem(where, NXC), y=lax.div(where, NXC))

    def z_peer(k):
        return spot(z=lax.rem(mz + k, NZR))

    def remote(src, dst, send_sem, recv_sem, where):
        return pltpu.make_async_remote_copy(
            src_ref=src, dst_ref=dst, send_sem=send_sem, recv_sem=recv_sem,
            device_id=where, device_id_type=MESH,
        )

    def group(copies, wholes, send_sem, recv_sem):
        for src, dst, where in copies:
            remote(src, dst, send_sem, recv_sem, where).start()
        return remote(wholes, wholes, send_sem, recv_sem, partner)

    body = pl.ds(1, ey)
    load_cot = pltpu.make_async_copy(cot_hbm, shifted.at[1, pl.ds(1, ex), body], load_sem.at[0])
    load_in = pltpu.make_async_copy(in_hbm, in_ref, load_sem.at[1])
    load_raw = pltpu.make_async_copy(raw_hbm, raw_ref, load_sem.at[2])
    load_cot.start()
    load_in.start()
    load_raw.start()

    low = {axis: me[axis] == 0 for axis in AXES}
    high = {axis: me[axis] == count[axis] - 1 for axis in AXES}
    plane_offs = [(a, b, 0) for a in (1, -1, 0) for b in (0, 1, -1) if (a, b) != (0, 0)]

    def neighbour(off):
        return {axis: lax.rem(me[axis] + count[axis] + o, count[axis]) for axis, o in zip(AXES, off)}

    def exists(off):
        ok = None
        for axis, o in zip(AXES, off):
            if o != 0:
                one = me[axis] < count[axis] - 1 if o > 0 else me[axis] > 0
                ok = one if ok is None else jnp.logical_and(ok, one)
        return ok

    barrier = pltpu.get_barrier_semaphore()
    for off in [(0, 0, 1), (0, 0, -1)] + plane_offs:

        @pl.when(exists(off))
        def _():
            pl.semaphore_signal(barrier, inc=1, device_id=neighbour(off), device_id_type=MESH)

    near_z = [spot(z=lax.rem(mz + k, NZR)) for k in (1, 2, NZR - 2, NZR - 1)]
    lines = [spot(c=c, x=x) for x in x_line for c in range(NCORE)]
    lines += [spot(c=c, y=y) for y in y_line for c in range(NCORE)]
    for where in near_z + lines:
        pl.semaphore_signal(barrier, inc=1, device_id=where, device_id_type=MESH)

    line_end = jnp.logical_or(zl == 0, zl == NZL - 1)

    @pl.when(line_end)
    def _():
        where = spot(z=zh * NZL + NZL - 1 - zl)
        pl.semaphore_signal(barrier, inc=1, device_id=where, device_id_type=MESH)

    def sides(axis):
        return (me[axis] > 0).astype(jnp.int32), (me[axis] < count[axis] - 1).astype(jnp.int32)

    around = (1 + sum(sides("gx"))) * (1 + sum(sides("gy")))
    greeted = around - 1 + sum(sides("gz")) + len(near_z) + len(lines) + line_end.astype(jnp.int32)

    tile = jnp.zeros((16, chan), BF16)
    for end, at_end in enumerate((low, high)):
        shifted[1, (ex + 1) * end] = jnp.zeros((ey + 2, ez, chan), BF16)
        shifted[1, :, (ey + 1) * end] = jnp.zeros((ex + 2, ez, chan), BF16)
        for side in range(2):
            halo_y[side, (ex + 1) * end] = tile

        @pl.when(at_end["gx"])
        def _():
            halo_x[end] = jnp.zeros((ey + 2, ez, chan), BF16)

        @pl.when(at_end["gy"])
        def _():
            for side in range(2):
                halo_x[side, (ey + 1) * end] = tile
            halo_y[end, 1:ex + 1] = jnp.zeros((ex, ez, chan), BF16)

        @pl.when(at_end["gz"])
        def _():
            in_in[end] = jnp.zeros((ex, ey, chan), BF16)
            along_in[end] = jnp.zeros((ex + 4, ey, chan), BF16)

    w_all[taps] = jnp.zeros((8, 16, chan), BF16)
    for y in range(NYC):
        send_xy[y, taps] = tile
    with jax.named_scope("w_cot"):
        load_cot.wait()

    load_in.wait()
    for x in range(ex):
        block = in_ref[x].astype(F32)
        in_out[0, x] = block[:, 0, :].astype(BF16)
        in_out[1, x] = block[:, ez - 1, :].astype(BF16)
    order = [t for c in (1, 2, 0) for t in range(c, taps, 3)]

    def per_output(value):
        return jnp.sum(jnp.sum(value, axis=0), axis=0, keepdims=True)

    load_raw.wait()
    raw = raw_ref[...]
    raw_sum = per_output(raw)
    slab = core * NYC + my
    stats_w[slab, zl] = jnp.concatenate([raw_sum, per_output(raw * raw)], axis=0)
    local_mean = raw_sum / float(rows * taps)
    for u, t in enumerate(order):
        wz[zl, u] = (raw_ref[t] - local_mean).astype(BF16)
    row_i = lax.broadcasted_iota(jnp.int32, (chan, chan), 0)
    col_i = lax.broadcasted_iota(jnp.int32, (chan, chan), 1)

    def natural(i):
        return (i // 4 % 4) * 32 + (i // 64) * 16 + (i // 16 % 4) * 4 + i % 4

    to_mine = jnp.where(col_i == natural(row_i), 1.0, 0.0).astype(BF16)
    to_natural = jnp.where(row_i == natural(col_i), 1.0, 0.0).astype(BF16)

    def transposed(block):
        return lax.dot_general(
            to_mine, block, (((1,), (1,)), ((), ())), preferred_element_type=F32
        ).astype(BF16)

    depth = lax.broadcasted_iota(jnp.int32, (ey, ez, chan), 1)
    for kind in range(3):
        ends = [[], []]
        for x in range(ex):
            block = in_ref[x]
            if kind:
                moved = pltpu.roll(block.astype(F32), ez - 1 if kind == 1 else 1, 1)
                block = jnp.where(depth == (ez - 1 if kind == 1 else 0), 0.0, moved).astype(BF16)
            in_t[kind, :, x * ey * ez:(x + 1) * ey * ez] = transposed(block.reshape(ey * ez, chan))
            ends[0].append(block[0])
            ends[1].append(block[ey - 1])
        for side in range(2):
            edge_y[side, kind] = transposed(jnp.concatenate(ends[side], axis=0))
    with jax.named_scope("w_barrier"):
        pl.semaphore_wait(barrier, greeted)

    def plane_copy(n, off):
        a, b, _ = off
        near = {1: (ex, ey), -1: (1, 1)}
        side = {1: 0, -1: 1}
        if b == 0:
            src, dst = shifted.at[1, near[a][0], body], halo_x.at[side[a], body]
        elif a == 0:
            src, dst = shifted.at[1, pl.ds(1, ex), near[b][1]], halo_y.at[side[b], pl.ds(1, ex)]
        else:
            src, dst = shifted.at[1, near[a][0], near[b][1]], halo_x.at[side[a], 0 if b > 0 else ey + 1]
        return remote(src, dst, sends.at[n], halo_recv.at[n], neighbour(off))

    def z_copies(n, source, target):
        pairs = []
        for f, off in ((1, (0, 0, 1)), (0, (0, 0, -1))):
            copy = remote(source.at[f], target.at[1 - f], sends.at[n + f], halo_recv.at[n + f], neighbour(off))
            pairs.append([(off, copy)])
        return pairs

    plane = [(off, plane_copy(n, off)) for n, off in enumerate(plane_offs)]
    in_lo, in_hi = z_copies(8, in_out, in_in)
    along = sum(z_copies(10, along_out, along_in), [])

    def halo_do(halos, act, flip):
        for off, copy in halos:

            @pl.when(exists(tuple(-o for o in off) if flip else off))
            def _():
                act(copy)

    def halo_start(halos):
        halo_do(halos, lambda copy: copy.start(), False)

    def halo_sent(halos):
        halo_do(halos, lambda copy: copy.wait_send(), False)

    def halo_wait(halos):
        halo_do(halos, lambda copy: copy.wait_recv(), True)

    halo_start(plane)
    halo_start(in_hi)
    halo_start(in_lo)
    w1_copies = []
    for k in range(1, NZL):
        where = spot(z=zh * NZL + lax.rem(zl + k, NZL))
        w1_copies.append((wz.at[zl], wz.at[zl], where))
    gather_z = group(w1_copies, wz.at[pl.ds(0, NZL - 1)], sends.at[21], recvs.at[9])
    stats_z = group(
        [(stats_w.at[slab, zl], stats_w.at[slab, zl], where) for _, _, where in w1_copies],
        stats_w.at[slab, pl.ds(0, NZL - 1)], sends.at[22], recvs.at[10],
    )
    for where in near_z + [spot(x=x) for x in x_line]:
        pl.semaphore_signal(hello, inc=1, device_id=where, device_id_type=MESH)

    def view(slot, t, start, planes):
        a, b = t // 9, (t // 3) % 3
        block = shifted[slot, pl.ds(start + 2 - a, planes), 2 - b:2 - b + ey]
        return block.reshape(planes * ey * ez, chan)

    half_rows = chan // NCORE
    kinds = {1: 0, 2: 1, 0: 2}

    def products(first, last, left, right_of):
        u = first
        while u < last:
            both = [u]
            if u + 1 < last and order[u + 1] % 3 == order[u] % 3:
                both.append(u + 1)
            views = [right_of(order[v]) for v in both]
            right = jnp.concatenate(views, axis=1) if len(views) > 1 else views[0]
            product = jnp.dot(left(order[u]), right, preferred_element_type=F32)
            for j, v in enumerate(both):
                for c in range(NCORE):
                    yield c, v, product[c * half_rows:(c + 1) * half_rows, j * chan:(j + 1) * chan]
            u += len(both)

    def filter_main(first, last):
        for c, v, value in products(first, last, lambda t: in_t[kinds[t % 3]], lambda t: view(1, t, 0, ex)):
            part[c, v] = value

    where_is = {t: v for v, t in enumerate(order)}
    tap_c = (1, 2, 0)

    def filter_side(left, rights, taps_of):
        product = jnp.dot(left, jnp.concatenate(rights, axis=1), preferred_element_type=F32)
        for kind in range(3):
            for j in range(3):
                v = where_is[taps_of(j) + tap_c[kind]]
                for c in range(NCORE):
                    low_row = kind * chan + c * half_rows
                    part[c, v] = part[c, v] + product[low_row:low_row + half_rows, j * chan:(j + 1) * chan]

    def filter_plane():
        for side, a, x in ((1, 0, ex - 1), (0, 2, 0)):
            left = in_t[:, :, x * ey * ez:(x + 1) * ey * ez].reshape(3 * chan, ey * ez)
            rights = [halo_x[side, 2 - b:2 - b + ey].reshape(ey * ez, chan) for b in range(3)]
            filter_side(left, rights, lambda b: a * 9 + b * 3)
        for side, b in ((1, 0), (0, 2)):
            left = edge_y[side].reshape(3 * chan, ex * ez)
            rights = [halo_y[side, 2 - a:2 - a + ex].reshape(ex * ez, chan) for a in range(3)]
            filter_side(left, rights, lambda a: a * 9 + b * 3)

    def fill_plane():
        for side in range(2):
            shifted[1, (ex + 1) * side] = halo_x[side]
            shifted[1, 1:ex + 1, (ey + 1) * side] = halo_y[side, 1:ex + 1]

    def make_rim():
        for x in range(ex + 2):
            plane = shifted[1, x].astype(F32)
            for side, z in enumerate((0, ez - 1)):
                rim[side, x, 0:ey + 2] = plane[:, z, :]
        for side in range(2):
            for b in range(3):
                rim_view[side, b] = rim[side, :, 2 - b:2 - b + ey].astype(BF16)
            along_out[side, 0:ex + 2] = rim_view[side, 1]
            for b in range(2):
                ends = jnp.concatenate([rim[side, :, (ey + 1) * b], jnp.zeros((ey - ex - 2, chan), F32)], axis=0)
                along_out[side, ex + 2 + b] = ends.astype(BF16)

    def filter_rim(side, first, last):
        edge_t[side] = transposed(in_in[side].reshape(ex * ey, chan))

        def rim_of(t):
            a, b = t // 9, (t // 3) % 3
            return rim_view[side, b, 2 - a:2 - a + ex].reshape(ex * ey, chan)

        for c, v, value in products(first, last, lambda t: edge_t[side], rim_of):
            part[c, v] = part[c, v] + value

    def core_chunk(n):
        first, done, _, _ = CHUNKS[n]
        span = pl.ds(first, done)
        return group(
            [(part.at[1 - core, span], recv_c.at[span], partner)], recv_c.at[span], sends.at[12 + n], recvs.at[n]
        )

    def xy_chunk(n, copy):
        first, done, each, slot = CHUNKS[n]
        with jax.named_scope("w_core%d" % n):
            copy.wait_recv()
        for v in range(first, first + done):
            total = part[core, v] + recv_c[v]
            for y in range(NYC):
                send_xy[y, v] = total[y * 16:(y + 1) * 16].astype(BF16)
        copies = []
        for k in range(1, NXC * NYC):
            px, py = xy_peer(k)
            copies.append((
                send_xy.at[py, pl.ds(first + px * each, each)], recv_xy.at[k - 1, pl.ds(slot, each)],
                spot(x=px, y=py),
            ))
        return group(copies, recv_xy.at[:, pl.ds(slot, each)], sends.at[15 + n], recvs.at[3 + n])

    def z_chunk(n, copy):
        first, done, each, slot = CHUNKS[n]
        with jax.named_scope("w_xy%d" % n):
            copy.wait_recv()
        span = pl.ds(slot, each)
        total = send_xy[my, pl.ds(first + mx * each, each)].astype(F32)
        for k in range(1, NXC * NYC):
            total = total + recv_xy[k - 1, span].astype(F32)
        recv_z[mz, span] = total.astype(BF16)
        return group(
            [(recv_z.at[mz, span], recv_z.at[mz, span], z_peer(k)) for k in range(1, NZR)],
            recv_z.at[pl.ds(0, NZR - 1), span], sends.at[18 + n], recvs.at[6 + n],
        )

    def shift(slot, side, amount, edge):
        depth = lax.broadcasted_iota(jnp.int32, (ey, ez, chan), 1)
        for x in range(ex + 2):
            plane = shifted[1, x, 1:ey + 1].astype(F32)
            outer = along_in[side, x].astype(F32)[:, None, :]
            shifted[slot, x, 1:ey + 1] = jnp.where(depth == edge, outer, pltpu.roll(plane, amount, 1)).astype(BF16)
        depth = lax.broadcasted_iota(jnp.int32, (ex + 2, ez, chan), 1)
        for b in range(2):
            y = (ey + 1) * b
            plane = shifted[1, :, y].astype(F32)
            outer = along_in[side, ex + 2 + b].astype(F32)[0:ex + 2][:, None, :]
            shifted[slot, :, y] = jnp.where(depth == edge, outer, pltpu.roll(plane, amount, 1)).astype(BF16)

    filter_main(0, taps)
    with jax.named_scope("w_halo_xy"):
        halo_wait(plane)
    filter_plane()
    core_0 = core_chunk(0)
    fill_plane()
    make_rim()
    with jax.named_scope("w_halo_hi"):
        halo_wait(in_hi)
    filter_rim(1, 9, 18)
    core_1 = core_chunk(1)
    with jax.named_scope("w_halo_lo"):
        halo_wait(in_lo)
    filter_rim(0, 18, 27)
    core_2 = core_chunk(2)
    with jax.named_scope("w_hello"):
        pl.semaphore_wait(hello, len(near_z) + len(x_line))
    xy_0 = xy_chunk(0, core_0)
    with jax.named_scope("w_gather_z"):
        gather_z.wait_recv()
        stats_z.wait_recv()
    for u in range(taps):
        w_all[u, slab] = wz[:, u].astype(F32).reshape(16, chan).astype(BF16)

    def gather_part(first, last, send, recv):
        span = pl.ds(first, last - first)
        return group(
            [(w_all.at[span, slab], w_all.at[span, slab], spot(y=y)) for y in y_line],
            w_all.at[span, pl.ds(0, NYC - 1)], sends.at[send], recvs.at[recv],
        )

    def share_part(first, last, send, recv):
        slabs = w_all.at[pl.ds(first, last - first), pl.ds(core * NYC, NYC)]
        return group([(slabs, slabs, partner)], slabs, sends.at[send], recvs.at[recv])

    gather_y = gather_part(0, W_SPLIT, 23, 11)
    stats_y = group(
        [(stats_w.at[slab], stats_w.at[slab], spot(y=y)) for y in y_line],
        stats_w.at[pl.ds(0, NYC - 1)], sends.at[24], recvs.at[12],
    )
    xy_1 = xy_chunk(1, core_1)
    xy_2 = xy_chunk(2, core_2)
    gather_y2 = gather_part(W_SPLIT, taps, 25, 17)
    halo_start(along)
    for halos in (plane, in_hi, in_lo):
        halo_sent(halos)
    z_0 = z_chunk(0, xy_0)
    with jax.named_scope("w_gather_y"):
        gather_y.wait_recv()
        stats_y.wait_recv()
    core_0.wait_send()
    core_1.wait_send()
    gather_c = share_part(0, W_SPLIT, 12, 13)
    mine = stats_w.at[pl.ds(core * NYC, NYC)]
    stats_c = group([(mine, mine, partner)], mine, sends.at[13], recvs.at[14])
    z_1 = z_chunk(1, xy_1)
    z_2 = z_chunk(2, xy_2)

    with jax.named_scope("w_gather_c"):
        gather_c.wait_recv()
        stats_c.wait_recv()
    sums = stats_w[0, 0]
    for k in range(1, 32):
        sums = sums + stats_w[k // NZL, k % NZL]
    mean_out = sums[0:1] / fan_count
    var_out = sums[1:2] / fan_count - mean_out * mean_out
    inv_std = lax.rsqrt(var_out + var_eps)
    offset = []
    for k in range(32):
        gap = stats_w[k // NZL, k % NZL][0:1] / float(rows * taps) - mean_out
        offset.append(jnp.broadcast_to(gap, (rows, chan)))
    offset = jnp.concatenate(offset, axis=0)

    def standardize(first, last):
        for u in range(first, last, 2):
            pair = range(u, min(u + 2, last))
            right = []
            for v in pair:
                value = (w_all[v].reshape(chan, chan).astype(F32) + offset) * inv_std
                right.append(value.astype(BF16))
            right = jnp.concatenate(right, axis=1) if len(right) > 1 else right[0]
            w_cat[:, u * chan:(u + len(pair)) * chan] = jnp.dot(
                to_natural, right, preferred_element_type=F32
            ).astype(BF16)

    def dx_steps(first, last, step, finish):
        def dx_step(n, carry):
            start = n * step
            left = jnp.concatenate([view(2 - t % 3, t, start, step) for t in order[first:last]], axis=1)
            product = lax.dot_general(
                left, w_cat[:, first * chan:last * chan], (((1,), (1,)), ((), ())), preferred_element_type=F32
            )
            finish(pl.ds(start, step), product.reshape(step, ey, ez, chan))
            return carry

        lax.fori_loop(0, ex // step, dx_step, 0)

    def keep(span, value):
        dx_acc[span] = value

    def finish(span, value):
        dx_ref[span] = (value + dx_acc[span]).astype(BF16)

    standardize(0, W_SPLIT)
    with jax.named_scope("dxa"):
        dx_steps(0, W_SPLIT, 2, keep)
    with jax.named_scope("w_gather_y2"):
        gather_y2.wait_recv()
    core_2.wait_send()
    gather_c2 = share_part(W_SPLIT, taps, 14, 18)

    with jax.named_scope("w_z"):
        z_0.wait_recv()
        z_1.wait_recv()
        z_2.wait_recv()
    grad = recv_z[0].astype(F32)
    for k in range(1, NZR):
        grad = grad + recv_z[k].astype(F32)
    pivot = stats_w[slab, 0][0:1]
    gap = [jnp.broadcast_to((stats_w[slab, q][0:1] - pivot) / float(rows * taps), (rows, chan)) for q in range(NZL)]
    gap = jnp.concatenate(gap, axis=0)
    near = []
    for first, _, each, _ in CHUNKS:
        near += [w_all[first + mx * each + j, slab].astype(F32) for j in range(each)]
    cross = grad[0] * (near[0] + gap)
    for j in range(1, SLOTS):
        cross = cross + grad[j] * (near[j] + gap)
    stats_g[flat_g] = jnp.concatenate(
        [per_output(grad), jnp.sum(cross, axis=0, keepdims=True), per_output(grad * grad), jnp.zeros((1, chan), F32)],
        axis=0,
    )
    xy_0.wait_send()
    xy_1.wait_send()
    grad_sums = group(
        [(stats_g.at[flat_g], stats_g.at[flat_g], stat_peer(k)) for k in range(1, 32)],
        stats_g.at[pl.ds(0, 31)], sends.at[15], recvs.at[15],
    )
    for j in range(SLOTS):
        owned = grad[j, 0:rows]
        for q in range(1, NZL):
            owned = jnp.where(zl == q, grad[j, q * rows:(q + 1) * rows], owned)
        full[mx, j] = owned
    gather_x = group(
        [(full.at[mx], full.at[mx], spot(x=x)) for x in x_line],
        full.at[pl.ds(0, NXC - 1)], sends.at[16], recvs.at[16],
    )

    with jax.named_scope("w_halo_along"):
        halo_wait(along)
        halo_sent(along)
    shift(2, 1, ez - 1, ez - 1)
    shift(0, 0, 1, 0)
    with jax.named_scope("w_gather_c2"):
        gather_c2.wait_recv()
    standardize(W_SPLIT, taps)
    with jax.named_scope("dxb"):
        dx_steps(W_SPLIT, taps, 2, finish)

    with jax.named_scope("w_grad_sums"):
        grad_sums.wait_recv()
    with jax.named_scope("w_gather_x"):
        gather_x.wait_recv()
    sum_grad, sum_cross, sum_square = (jnp.zeros((1, chan), F32) for _ in range(3))
    for k in range(32):
        one = stats_g[k]
        about = stats_w[k % NCORE * NYC + k // (NXC * NCORE), 0][0:1] / float(rows * taps) - mean_out
        sum_grad = sum_grad + one[0:1]
        sum_cross = sum_cross + (one[1:2] + about * one[0:1])
        sum_square = sum_square + one[2:3]
    sum_cross = sum_cross * inv_std
    mean_grad = sum_grad / fan_count
    mean_cross = sum_cross / fan_count
    spread = sum_square - 2.0 * mean_grad * sum_grad - 2.0 * mean_cross * sum_cross
    spread = (
        spread
        + fan_count * mean_grad * mean_grad
        + fan_count * mean_cross * mean_cross * var_out / (var_out + var_eps)
    )
    square_sum = jnp.sum(inv_std * inv_std * spread, axis=1, keepdims=True)
    scale = jnp.minimum(1.0, clip_norm * lax.rsqrt(square_sum + norm_eps))
    factor = inv_std * scale
    for first, done, each, slot in CHUNKS:
        for v in range(done):
            t = order[first + v]
            std = (raw_ref[t] - mean_out) * inv_std
            wg_ref[t] = factor * (full[v // each, slot + v % each] - mean_grad - std * mean_cross)

    with jax.named_scope("w_sends"):
        for copy in (
            xy_2, gather_z, stats_z, gather_y, gather_y2, stats_y, gather_c, gather_c2, stats_c, z_0, z_1, z_2,
            grad_sums, gather_x,
        ):
            copy.wait_send()


def write_out(dx_ref, wg_ref, dx_hbm, wg_hbm, sem):
    copies = [pltpu.make_async_copy(dx_ref, dx_hbm, sem.at[0]), pltpu.make_async_copy(wg_ref, wg_hbm, sem.at[1])]
    for copy in copies:
        copy.start()
    for copy in copies:
        copy.wait()


def on_device(raw_weight, inputs, cotangent):
    rows, taps, chan = raw_weight.shape
    ex, ey, ez = inputs.shape[:3]
    dma = pltpu.SemaphoreType.DMA

    scratch = [
        pltpu.VMEM((taps, rows, chan), F32),
        pltpu.VMEM(inputs.shape, BF16),
        pltpu.VMEM((3, ex + 2, ey + 2, ez, chan), BF16),
        pltpu.VMEM((2, ey + 2, ez, chan), BF16),
        pltpu.VMEM((2, ex + 2, ez, chan), BF16),
        pltpu.VMEM((2, ex + 4, ey, chan), BF16),
        pltpu.VMEM((2, ex + 4, ey, chan), BF16),
        pltpu.VMEM((2, ex, ey, chan), BF16),
        pltpu.VMEM((2, ex, ey, chan), BF16),
        pltpu.VMEM((3, chan, ex * ey * ez), BF16),
        pltpu.VMEM((2, 3, chan, ex * ez), BF16),
        pltpu.VMEM((2, chan, ex * ey), BF16),
        pltpu.VMEM((2, ex + 2, 24, chan), F32),
        pltpu.VMEM((2, 3, ex + 2, ey, chan), BF16),
        pltpu.VMEM((NCORE, taps, chan // NCORE, chan), F32),
        pltpu.VMEM((taps, chan // NCORE, chan), F32),
        pltpu.VMEM((NYC, taps + 1, 16, chan), BF16),
        pltpu.VMEM((NXC * NYC - 1, SLOTS, 16, chan), BF16),
        pltpu.VMEM((NZR, SLOTS, 16, chan), BF16),
        pltpu.VMEM((NXC, SLOTS, rows, chan), F32),
        pltpu.VMEM((NZL, taps, rows, chan), BF16),
        pltpu.VMEM((taps + 1, 8, 16, chan), BF16),
        pltpu.VMEM((chan, taps * chan), BF16),
        pltpu.VMEM(inputs.shape, F32),
        pltpu.VMEM((8, NZL, 2, chan), F32),
        pltpu.VMEM((32, 4, chan), F32),
        dma((3,)), dma((26,)), dma((12,)), dma((19,)), pltpu.SemaphoreType.REGULAR,
    ]
    vmem = pl.BlockSpec(memory_space=pltpu.VMEM)
    anywhere = pl.BlockSpec(memory_space=pl.ANY)
    shapes = (
        jax.ShapeDtypeStruct(cotangent.shape, BF16),
        jax.ShapeDtypeStruct((taps, rows, chan), F32),
    )
    results = pl.pallas_call(
        kernel,
        out_shape=tuple(pltpu.VMEM(one.shape, one.dtype) for one in shapes),
        in_specs=[anywhere] * 3,
        out_specs=(vmem, vmem),
        scratch_shapes=scratch,
        compiler_params=pltpu.CompilerParams(
            collective_id=0, has_side_effects=True, vmem_limit_bytes=32 * 1024 * 1024
        ),
    )(*(
        pltpu.with_memory_space_constraint(one, pltpu.HBM)
        for one in (jnp.transpose(raw_weight, (1, 0, 2)), inputs, cotangent)
    ))
    input_grad, weight_grad = pl.pallas_call(
        write_out,
        out_shape=shapes,
        in_specs=[vmem, vmem],
        out_specs=(anywhere, anywhere),
        scratch_shapes=[dma((2,))],
    )(*(pltpu.with_memory_space_constraint(one, pltpu.VMEM) for one in results))
    return input_grad, jnp.transpose(weight_grad, (1, 0, 2))


def solution(mesh):
    in_specs = (P(("gx", "gy"), None, None), P("gx", "gy", "gz", None), P("gx", "gy", "gz", None))
    out_specs = (P("gx", "gy", "gz", None), P(("gx", "gy"), None, None))
    return jax.shard_map(
        on_device, mesh=mesh, in_specs=in_specs, out_specs=out_specs, check_vma=False
    )
```

time: 38.9 us -> 38.5 us (0.990)
  Pallas kernels: 38.2 us -> 37.7 us
    pallas_call x1, Pallas kernels: 37.3 us -> 36.9 us  [on_device(): pl.pallas_call(kernel, out_shape=tuple((pltpu.VMEM(one.shape, one.dtype)...]
where the time goes in v5:
time: 38.5 us; the launch traced here: 38.4 us
  Pallas kernels  37.7 us (98%)
  between operations  0.64 us (2%)
    pallas_call x1, Pallas kernels, on_device(): pl.pallas_call(kernel, out_shape=tuple((pltpu.VMEM(one.shape, one.dtype)...  36.9 us
    pallas_call x1, Pallas kernels, on_device(): pl.pallas_call(write_out, out_shape=shapes, in_specs=[vmem, vmem], out_sp...  0.81 us

profile of v5, /device:TPU:1, one launch (start us, length us, event | category | flops | bytes accessed | tf_op | source)
XLA Modules:
  0.0 38.4 jit_solution(12966285402168478048)
XLA Ops:
  0.6 36.9 %shard_map.50 = (bf16[8,16,16,128]{3,2,1,0:T(8,128)(2,1)S(1)}, f32[27,4,128]{2,1,0:T(4,128)S(1)}) custom-call(f32[27,4,128]{2,1,0:T(4,128)} %bitcast.2, bf16[8,16,16,128]{3,2,1,0:T(8,128)(2,1)} %in_hbm.1, bf16[8,16,16,128]{3,2,1,0:T(8,128)(2,1)} %cot_hbm.1), custom_call_target="tpu_custom_call" | custom-call | tf_op jit(solution)/shard_map/pallas_call | solution.py:624
  37.6 0.8 %shard_map.51 = (bf16[8,16,16,128]{3,2,1,0:T(8,128)(2,1)}, f32[27,4,128]{2,1,0:T(4,128)}) custom-call(bf16[8,16,16,128]{3,2,1,0:T(8,128)(2,1)S(1)} %get-tuple-element.6.dx_ref, f32[27,4,128]{2,1,0:T(4,128)S(1)} %get-tuple-element.7.wg_ref), custom_call_target="tpu_custom_call" | custom-call | tf_op jit(solution)/shard_map/pallas_call | solution.py:637

commit v6 on v5

--- a/solution.py
+++ b/solution.py
@@ -19,12 +19,12 @@
 NZR = NZL * NZH
 CHUNKS = ((0, 8, 2, 0), (8, 8, 2, 2), (16, 11, 3, 4))
 SLOTS = 7
-W_SPLIT = 9
+W_SPLIT = 11
 
 
 def kernel(raw_hbm, in_hbm, cot_hbm, dx_ref, wg_ref, *scratch):
-    (raw_ref, in_ref, shifted, halo_x, halo_y, along_out, along_in, in_out, in_in, in_t, edge_y, edge_t, rim, rim_view,
-     part, recv_c, send_xy, recv_xy, recv_z, full, wz, w_all, w_cat, dx_acc, stats_w, stats_g,
+    (raw_ref, in_ref, shifted, halo_x, halo_y, along_out, along_in, in_out, in_in, in_t, edge_y, rim, rim_view,
+     part, recv_c, send_xy, recv_xy, recv_z, full, wy, wz, w_all, w_cat, dx_acc, stats_w, stats_g,
      load_sem, sends, halo_recv, recvs, hello) = scratch
     taps, rows, chan = raw_ref.shape
     ex, ey, ez = in_ref.shape[:3]
@@ -140,7 +140,7 @@
 
         @pl.when(at_end["gz"])
         def _():
-            in_in[end] = jnp.zeros((ex, ey, chan), BF16)
+            in_in[end] = jnp.zeros((chan, ex * ey), BF16)
             along_in[end] = jnp.zeros((ex + 4, ey, chan), BF16)
 
     w_all[taps] = jnp.zeros((8, 16, chan), BF16)
@@ -150,15 +150,75 @@
         load_cot.wait()
 
     load_in.wait()
-    for x in range(ex):
-        block = in_ref[x].astype(F32)
-        in_out[0, x] = block[:, 0, :].astype(BF16)
-        in_out[1, x] = block[:, ez - 1, :].astype(BF16)
     order = [t for c in (1, 2, 0) for t in range(c, taps, 3)]
 
     def per_output(value):
         return jnp.sum(jnp.sum(value, axis=0), axis=0, keepdims=True)
 
+    row_i = lax.broadcasted_iota(jnp.int32, (chan, chan), 0)
+    col_i = lax.broadcasted_iota(jnp.int32, (chan, chan), 1)
+
+    def natural(i):
+        return (i // 4 % 4) * 32 + (i // 64) * 16 + (i // 16 % 4) * 4 + i % 4
+
+    to_mine = jnp.where(col_i == natural(row_i), 1.0, 0.0).astype(BF16)
+    to_natural = jnp.where(row_i == natural(col_i), 1.0, 0.0).astype(BF16)
+
+    def transposed(block):
+        return lax.dot_general(
+            to_mine, block, (((1,), (1,)), ((), ())), preferred_element_type=F32
+        ).astype(BF16)
+
+    for f, z in enumerate((0, ez - 1)):
+        face = [in_ref[x].astype(F32)[:, z, :] for x in range(ex)]
+        in_out[f] = transposed(jnp.concatenate(face, axis=0).astype(BF16))
+    with jax.named_scope("w_barrier"):
+        pl.semaphore_wait(barrier, greeted)
+
+    def plane_copy(n, off):
+        a, b, _ = off
+        near = {1: (ex, ey), -1: (1, 1)}
+        side = {1: 0, -1: 1}
+        if b == 0:
+            src, dst = shifted.at[1, near[a][0], body], halo_x.at[side[a], body]
+        elif a == 0:
+            src, dst = shifted.at[1, pl.ds(1, ex), near[b][1]], halo_y.at[side[b], pl.ds(1, ex)]
+        else:
+            src, dst = shifted.at[1, near[a][0], near[b][1]], halo_x.at[side[a], 0 if b > 0 else ey + 1]
+        return remote(src, dst, sends.at[n], halo_recv.at[n], neighbour(off))
+
+    def z_copies(n, source, target):
+        pairs = []
+        for f, off in ((1, (0, 0, 1)), (0, (0, 0, -1))):
+            copy = remote(source.at[f], target.at[1 - f], sends.at[n + f], halo_recv.at[n + f], neighbour(off))
+            pairs.append([(off, copy)])
+        return pairs
+
+    plane = [(off, plane_copy(n, off)) for n, off in enumerate(plane_offs)]
+    in_lo, in_hi = z_copies(8, in_out, in_in)
+    along = sum(z_copies(10, along_out, along_in), [])
+
+    def halo_do(halos, act, flip):
+        for off, copy in halos:
+
+            @pl.when(exists(tuple(-o for o in off) if flip else off))
+            def _():
+                act(copy)
+
+    def halo_start(halos):
+        halo_do(halos, lambda copy: copy.start(), False)
+
+    def halo_sent(halos):
+        halo_do(halos, lambda copy: copy.wait_send(), False)
+
+    def halo_wait(halos):
+        halo_do(halos, lambda copy: copy.wait_recv(), True)
+
+    halo_start(in_hi)
+    halo_start(in_lo)
+    halo_start(plane)
+    for where in near_z + [spot(x=x) for x in x_line]:
+        pl.semaphore_signal(hello, inc=1, device_id=where, device_id_type=MESH)
     load_raw.wait()
     raw = raw_ref[...]
     raw_sum = per_output(raw)
@@ -166,21 +226,23 @@
     stats_w[slab, zl] = jnp.concatenate([raw_sum, per_output(raw * raw)], axis=0)
     local_mean = raw_sum / float(rows * taps)
     for u, t in enumerate(order):
-        wz[zl, u] = (raw_ref[t] - local_mean).astype(BF16)
-    row_i = lax.broadcasted_iota(jnp.int32, (chan, chan), 0)
-    col_i = lax.broadcasted_iota(jnp.int32, (chan, chan), 1)
-
-    def natural(i):
-        return (i // 4 % 4) * 32 + (i // 64) * 16 + (i // 16 % 4) * 4 + i % 4
-
-    to_mine = jnp.where(col_i == natural(row_i), 1.0, 0.0).astype(BF16)
-    to_natural = jnp.where(row_i == natural(col_i), 1.0, 0.0).astype(BF16)
-
-    def transposed(block):
-        return lax.dot_general(
-            to_mine, block, (((1,), (1,)), ((), ())), preferred_element_type=F32
-        ).astype(BF16)
-
+        value = (raw_ref[t] - local_mean).astype(BF16)
+        if u < W_SPLIT:
+            wy[my, u] = value
+        else:
+            wz[zl, u - W_SPLIT] = value
+    w1_copies = []
+    for k in range(1, NZL):
+        where = spot(z=zh * NZL + lax.rem(zl + k, NZL))
+        w1_copies.append((wz.at[zl], wz.at[zl], where))
+    gather_z = group(w1_copies, wz.at[pl.ds(0, NZL - 1)], sends.at[21], recvs.at[9])
+    stats_z = group(
+        [(stats_w.at[slab, zl], stats_w.at[slab, zl], where) for _, _, where in w1_copies],
+        stats_w.at[slab, pl.ds(0, NZL - 1)], sends.at[22], recvs.at[10],
+    )
+    early_y = group(
+        [(wy.at[my], wy.at[my], spot(y=y)) for y in y_line], wy.at[pl.ds(0, NYC - 1)], sends.at[23], recvs.at[11]
+    )
     depth = lax.broadcasted_iota(jnp.int32, (ey, ez, chan), 1)
     for kind in range(3):
         ends = [[], []]
@@ -194,62 +256,6 @@
             ends[1].append(block[ey - 1])
         for side in range(2):
             edge_y[side, kind] = transposed(jnp.concatenate(ends[side], axis=0))
-    with jax.named_scope("w_barrier"):
-        pl.semaphore_wait(barrier, greeted)
-
-    def plane_copy(n, off):
-        a, b, _ = off
-        near = {1: (ex, ey), -1: (1, 1)}
-        side = {1: 0, -1: 1}
-        if b == 0:
-            src, dst = shifted.at[1, near[a][0], body], halo_x.at[side[a], body]
-        elif a == 0:
-            src, dst = shifted.at[1, pl.ds(1, ex), near[b][1]], halo_y.at[side[b], pl.ds(1, ex)]
-        else:
-            src, dst = shifted.at[1, near[a][0], near[b][1]], halo_x.at[side[a], 0 if b > 0 else ey + 1]
-        return remote(src, dst, sends.at[n], halo_recv.at[n], neighbour(off))
-
-    def z_copies(n, source, target):
-        pairs = []
-        for f, off in ((1, (0, 0, 1)), (0, (0, 0, -1))):
-            copy = remote(source.at[f], target.at[1 - f], sends.at[n + f], halo_recv.at[n + f], neighbour(off))
-            pairs.append([(off, copy)])
-        return pairs
-
-    plane = [(off, plane_copy(n, off)) for n, off in enumerate(plane_offs)]
-    in_lo, in_hi = z_copies(8, in_out, in_in)
-    along = sum(z_copies(10, along_out, along_in), [])
-
-    def halo_do(halos, act, flip):
-        for off, copy in halos:
-
-            @pl.when(exists(tuple(-o for o in off) if flip else off))
-            def _():
-                act(copy)
-
-    def halo_start(halos):
-        halo_do(halos, lambda copy: copy.start(), False)
-
-    def halo_sent(halos):
-        halo_do(halos, lambda copy: copy.wait_send(), False)
-
-    def halo_wait(halos):
-        halo_do(halos, lambda copy: copy.wait_recv(), True)
-
-    halo_start(plane)
-    halo_start(in_hi)
-    halo_start(in_lo)
-    w1_copies = []
-    for k in range(1, NZL):
-        where = spot(z=zh * NZL + lax.rem(zl + k, NZL))
-        w1_copies.append((wz.at[zl], wz.at[zl], where))
-    gather_z = group(w1_copies, wz.at[pl.ds(0, NZL - 1)], sends.at[21], recvs.at[9])
-    stats_z = group(
-        [(stats_w.at[slab, zl], stats_w.at[slab, zl], where) for _, _, where in w1_copies],
-        stats_w.at[slab, pl.ds(0, NZL - 1)], sends.at[22], recvs.at[10],
-    )
-    for where in near_z + [spot(x=x) for x in x_line]:
-        pl.semaphore_signal(hello, inc=1, device_id=where, device_id_type=MESH)
 
     def view(slot, t, start, planes):
         a, b = t // 9, (t // 3) % 3
@@ -318,13 +324,11 @@
                 along_out[side, ex + 2 + b] = ends.astype(BF16)
 
     def filter_rim(side, first, last):
-        edge_t[side] = transposed(in_in[side].reshape(ex * ey, chan))
-
         def rim_of(t):
             a, b = t // 9, (t // 3) % 3
             return rim_view[side, b, 2 - a:2 - a + ex].reshape(ex * ey, chan)
 
-        for c, v, value in products(first, last, lambda t: edge_t[side], rim_of):
+        for c, v, value in products(first, last, lambda t: in_in[side], rim_of):
             part[c, v] = part[c, v] + value
 
     def core_chunk(n):
@@ -399,8 +403,17 @@
     with jax.named_scope("w_gather_z"):
         gather_z.wait_recv()
         stats_z.wait_recv()
-    for u in range(taps):
-        w_all[u, slab] = wz[:, u].astype(F32).reshape(16, chan).astype(BF16)
+        early_y.wait_recv()
+    early_slab = core * NZL + zl
+    early = pl.ds(0, W_SPLIT)
+    for u in range(W_SPLIT):
+        w_all[u, early_slab] = wy[:, u].astype(F32).reshape(16, chan).astype(BF16)
+    for u in range(W_SPLIT, taps):
+        w_all[u, slab] = wz[:, u - W_SPLIT].astype(F32).reshape(16, chan).astype(BF16)
+    early_z = group(
+        [(w_all.at[early, early_slab], w_all.at[early, early_slab], where) for _, _, where in w1_copies],
+        w_all.at[early, pl.ds(0, NZL - 1)], sends.at[26], recvs.at[19],
+    )
 
     def gather_part(first, last, send, recv):
         span = pl.ds(first, last - first)
@@ -413,29 +426,33 @@
         slabs = w_all.at[pl.ds(first, last - first), pl.ds(core * NYC, NYC)]
         return group([(slabs, slabs, partner)], slabs, sends.at[send], recvs.at[recv])
 
-    gather_y = gather_part(0, W_SPLIT, 23, 11)
     stats_y = group(
         [(stats_w.at[slab], stats_w.at[slab], spot(y=y)) for y in y_line],
         stats_w.at[pl.ds(0, NYC - 1)], sends.at[24], recvs.at[12],
     )
     xy_1 = xy_chunk(1, core_1)
     xy_2 = xy_chunk(2, core_2)
-    gather_y2 = gather_part(W_SPLIT, taps, 25, 17)
     halo_start(along)
     for halos in (plane, in_hi, in_lo):
         halo_sent(halos)
     z_0 = z_chunk(0, xy_0)
+    gather_y2 = gather_part(W_SPLIT, taps, 25, 17)
+    z_1 = z_chunk(1, xy_1)
+    z_2 = z_chunk(2, xy_2)
     with jax.named_scope("w_gather_y"):
-        gather_y.wait_recv()
+        early_z.wait_recv()
         stats_y.wait_recv()
     core_0.wait_send()
     core_1.wait_send()
     gather_c = share_part(0, W_SPLIT, 12, 13)
     mine = stats_w.at[pl.ds(core * NYC, NYC)]
     stats_c = group([(mine, mine, partner)], mine, sends.at[13], recvs.at[14])
-    z_1 = z_chunk(1, xy_1)
-    z_2 = z_chunk(2, xy_2)
-
+
+    with jax.named_scope("w_halo_along"):
+        halo_wait(along)
+        halo_sent(along)
+    shift(2, 1, ez - 1, ez - 1)
+    shift(0, 0, 1, 0)
     with jax.named_scope("w_gather_c"):
         gather_c.wait_recv()
         stats_c.wait_recv()
@@ -451,6 +468,17 @@
         offset.append(jnp.broadcast_to(gap, (rows, chan)))
     offset = jnp.concatenate(offset, axis=0)
 
+    natural_slabs = [g % NCORE * NZL + g // NCORE for g in range(NCORE * NZL)]
+    early_offset = []
+    for g in range(NCORE * NZL):
+        for y in range(NYC):
+            gap = stats_w[g % NCORE * NYC + y, g // NCORE][0:1] / float(rows * taps) - mean_out
+            early_offset.append(jnp.broadcast_to(gap, (rows, chan)))
+    early_offset = jnp.concatenate(early_offset, axis=0)
+    for u in range(W_SPLIT):
+        value = jnp.concatenate([w_all[u, g] for g in natural_slabs], axis=0).astype(F32)
+        w_cat[:, u * chan:(u + 1) * chan] = ((value + early_offset) * inv_std).astype(BF16)
+
     def standardize(first, last):
         for u in range(first, last, 2):
             pair = range(u, min(u + 2, last))
@@ -481,32 +509,51 @@
     def finish(span, value):
         dx_ref[span] = (value + dx_acc[span]).astype(BF16)
 
-    standardize(0, W_SPLIT)
     with jax.named_scope("dxa"):
-        dx_steps(0, W_SPLIT, 2, keep)
+        dx_steps(0, W_SPLIT, 4, keep)
     with jax.named_scope("w_gather_y2"):
         gather_y2.wait_recv()
     core_2.wait_send()
     gather_c2 = share_part(W_SPLIT, taps, 14, 18)
 
-    with jax.named_scope("w_z"):
-        z_0.wait_recv()
-        z_1.wait_recv()
-        z_2.wait_recv()
-    grad = recv_z[0].astype(F32)
-    for k in range(1, NZR):
-        grad = grad + recv_z[k].astype(F32)
     pivot = stats_w[slab, 0][0:1]
     gap = [jnp.broadcast_to((stats_w[slab, q][0:1] - pivot) / float(rows * taps), (rows, chan)) for q in range(NZL)]
     gap = jnp.concatenate(gap, axis=0)
+    def own_rows(u):
+        pieces = []
+        for q in range(NZL):
+            block = w_all[u, core * NZL + q].astype(F32)
+            piece = block[0:rows]
+            for y in range(1, NYC):
+                piece = jnp.where(my == y, block[y * rows:(y + 1) * rows], piece)
+            pieces.append(piece)
+        return jnp.concatenate(pieces, axis=0)
+
     near = []
-    for first, _, each, _ in CHUNKS:
-        near += [w_all[first + mx * each + j, slab].astype(F32) for j in range(each)]
-    cross = grad[0] * (near[0] + gap)
+    for first, done, each, _ in CHUNKS:
+        for j in range(each):
+            u = first + mx * each + j
+            if first + done <= W_SPLIT:
+                near.append(own_rows(u))
+            elif first >= W_SPLIT:
+                near.append(w_all[u, slab].astype(F32))
+            else:
+                near.append(jnp.where(u < W_SPLIT, own_rows(u), w_all[u, slab].astype(F32)))
+    near = [value + gap for value in near]
+    grad = []
+    with jax.named_scope("w_z"):
+        for (_, _, each, slot), copy in zip(CHUNKS, (z_0, z_1, z_2)):
+            copy.wait_recv()
+            for j in range(slot, slot + each):
+                total = recv_z[0, j].astype(F32)
+                for k in range(1, NZR):
+                    total = total + recv_z[k, j].astype(F32)
+                grad.append(total)
+    total, cross, square = grad[0], grad[0] * near[0], grad[0] * grad[0]
     for j in range(1, SLOTS):
-        cross = cross + grad[j] * (near[j] + gap)
+        total, cross, square = total + grad[j], cross + grad[j] * near[j], square + grad[j] * grad[j]
     stats_g[flat_g] = jnp.concatenate(
-        [per_output(grad), jnp.sum(cross, axis=0, keepdims=True), per_output(grad * grad), jnp.zeros((1, chan), F32)],
+        [jnp.sum(value, axis=0, keepdims=True) for value in (total, cross, square)] + [jnp.zeros((1, chan), F32)],
         axis=0,
     )
     xy_0.wait_send()
@@ -516,25 +563,20 @@
         stats_g.at[pl.ds(0, 31)], sends.at[15], recvs.at[15],
     )
     for j in range(SLOTS):
-        owned = grad[j, 0:rows]
+        owned = grad[j][0:rows]
         for q in range(1, NZL):
-            owned = jnp.where(zl == q, grad[j, q * rows:(q + 1) * rows], owned)
+            owned = jnp.where(zl == q, grad[j][q * rows:(q + 1) * rows], owned)
         full[mx, j] = owned
     gather_x = group(
         [(full.at[mx], full.at[mx], spot(x=x)) for x in x_line],
         full.at[pl.ds(0, NXC - 1)], sends.at[16], recvs.at[16],
     )
 
-    with jax.named_scope("w_halo_along"):
-        halo_wait(along)
-        halo_sent(along)
-    shift(2, 1, ez - 1, ez - 1)
-    shift(0, 0, 1, 0)
     with jax.named_scope("w_gather_c2"):
         gather_c2.wait_recv()
     standardize(W_SPLIT, taps)
     with jax.named_scope("dxb"):
-        dx_steps(W_SPLIT, taps, 2, finish)
+        dx_steps(W_SPLIT, taps, 4, finish)
 
     with jax.named_scope("w_grad_sums"):
         grad_sums.wait_recv()
@@ -567,7 +609,7 @@
 
     with jax.named_scope("w_sends"):
         for copy in (
-            xy_2, gather_z, stats_z, gather_y, gather_y2, stats_y, gather_c, gather_c2, stats_c, z_0, z_1, z_2,
+            xy_2, gather_z, stats_z, early_y, early_z, gather_y2, stats_y, gather_c, gather_c2, stats_c, z_0, z_1, z_2,
             grad_sums, gather_x,
         ):
             copy.wait_send()
@@ -594,11 +636,10 @@
         pltpu.VMEM((2, ex + 2, ez, chan), BF16),
         pltpu.VMEM((2, ex + 4, ey, chan), BF16),
         pltpu.VMEM((2, ex + 4, ey, chan), BF16),
-        pltpu.VMEM((2, ex, ey, chan), BF16),
-        pltpu.VMEM((2, ex, ey, chan), BF16),
+        pltpu.VMEM((2, chan, ex * ey), BF16),
+        pltpu.VMEM((2, chan, ex * ey), BF16),
         pltpu.VMEM((3, chan, ex * ey * ez), BF16),
         pltpu.VMEM((2, 3, chan, ex * ez), BF16),
-        pltpu.VMEM((2, chan, ex * ey), BF16),
         pltpu.VMEM((2, ex + 2, 24, chan), F32),
         pltpu.VMEM((2, 3, ex + 2, ey, chan), BF16),
         pltpu.VMEM((NCORE, taps, chan // NCORE, chan), F32),
@@ -607,13 +648,14 @@
         pltpu.VMEM((NXC * NYC - 1, SLOTS, 16, chan), BF16),
         pltpu.VMEM((NZR, SLOTS, 16, chan), BF16),
         pltpu.VMEM((NXC, SLOTS, rows, chan), F32),
-        pltpu.VMEM((NZL, taps, rows, chan), BF16),
+        pltpu.VMEM((NYC, W_SPLIT, rows, chan), BF16),
+        pltpu.VMEM((NZL, taps - W_SPLIT, rows, chan), BF16),
         pltpu.VMEM((taps + 1, 8, 16, chan), BF16),
         pltpu.VMEM((chan, taps * chan), BF16),
         pltpu.VMEM(inputs.shape, F32),
         pltpu.VMEM((8, NZL, 2, chan), F32),
         pltpu.VMEM((32, 4, chan), F32),
-        dma((3,)), dma((26,)), dma((12,)), dma((19,)), pltpu.SemaphoreType.REGULAR,
+        dma((3,)), dma((27,)), dma((12,)), dma((20,)), pltpu.SemaphoreType.REGULAR,
     ]
     vmem = pl.BlockSpec(memory_space=pltpu.VMEM)
     anywhere = pl.BlockSpec(memory_space=pl.ANY)

time: 38.5 us -> 38.1 us (0.990)
  no operation moved by 1% of the time
where the time goes in v6:
time: 38.1 us; the launch traced here: 38 us
  Pallas kernels  37.4 us (98%)
  between operations  0.64 us (2%)
    pallas_call x1, Pallas kernels, on_device(): pl.pallas_call(kernel, out_shape=tuple((pltpu.VMEM(one.shape, one.dtype)...  36.6 us
    pallas_call x1, Pallas kernels, on_device(): pl.pallas_call(write_out, out_shape=shapes, in_specs=[vmem, vmem], out_sp...  0.81 us

profile of v6, /device:TPU:1, one launch (start us, length us, event | category | flops | bytes accessed | tf_op | source)
XLA Modules:
  0.0 38.0 jit_solution(12391242971873332271)
XLA Ops:
  0.6 36.6 %shard_map.50 = (bf16[8,16,16,128]{3,2,1,0:T(8,128)(2,1)S(1)}, f32[27,4,128]{2,1,0:T(4,128)S(1)}) custom-call(f32[27,4,128]{2,1,0:T(4,128)} %bitcast.2, bf16[8,16,16,128]{3,2,1,0:T(8,128)(2,1)} %in_hbm.1, bf16[8,16,16,128]{3,2,1,0:T(8,128)(2,1)} %cot_hbm.1), custom_call_target="tpu_custom_call" | custom-call | tf_op jit(solution)/shard_map/pallas_call | solution.py:666
  37.2 0.8 %shard_map.51 = (bf16[8,16,16,128]{3,2,1,0:T(8,128)(2,1)}, f32[27,4,128]{2,1,0:T(4,128)}) custom-call(bf16[8,16,16,128]{3,2,1,0:T(8,128)(2,1)S(1)} %get-tuple-element.6.dx_ref, f32[27,4,128]{2,1,0:T(4,128)S(1)} %get-tuple-element.7.wg_ref), custom_call_target="tpu_custom_call" | custom-call | tf_op jit(solution)/shard_map/pallas_call | solution.py:679

commit v7 on v6

--- a/solution.py
+++ b/solution.py
@@ -24,7 +24,7 @@
 
 def kernel(raw_hbm, in_hbm, cot_hbm, dx_ref, wg_ref, *scratch):
     (raw_ref, in_ref, shifted, halo_x, halo_y, along_out, along_in, in_out, in_in, in_t, edge_y, rim, rim_view,
-     part, recv_c, send_xy, recv_xy, recv_z, full, wy, wz, w_all, w_cat, dx_acc, stats_w, stats_g,
+     part, part_out, recv_c, send_xy, recv_xy, recv_z, full, wy, wz, w_all, w_cat, dx_acc, stats_w, stats_g,
      load_sem, sends, halo_recv, recvs, hello) = scratch
     taps, rows, chan = raw_ref.shape
     ex, ey, ez = in_ref.shape[:3]
@@ -334,8 +334,9 @@
     def core_chunk(n):
         first, done, _, _ = CHUNKS[n]
         span = pl.ds(first, done)
+        part_out[span] = part[1 - core, span].astype(BF16)
         return group(
-            [(part.at[1 - core, span], recv_c.at[span], partner)], recv_c.at[span], sends.at[12 + n], recvs.at[n]
+            [(part_out.at[span], recv_c.at[span], partner)], recv_c.at[span], sends.at[12 + n], recvs.at[n]
         )
 
     def xy_chunk(n, copy):
@@ -343,7 +344,7 @@
         with jax.named_scope("w_core%d" % n):
             copy.wait_recv()
         for v in range(first, first + done):
-            total = part[core, v] + recv_c[v]
+            total = part[core, v] + recv_c[v].astype(F32)
             for y in range(NYC):
                 send_xy[y, v] = total[y * 16:(y + 1) * 16].astype(BF16)
         copies = []
@@ -643,7 +644,8 @@
         pltpu.VMEM((2, ex + 2, 24, chan), F32),
         pltpu.VMEM((2, 3, ex + 2, ey, chan), BF16),
         pltpu.VMEM((NCORE, taps, chan // NCORE, chan), F32),
-        pltpu.VMEM((taps, chan // NCORE, chan), F32),
+        pltpu.VMEM((taps, chan // NCORE, chan), BF16),
+        pltpu.VMEM((taps, chan // NCORE, chan), BF16),
         pltpu.VMEM((NYC, taps + 1, 16, chan), BF16),
         pltpu.VMEM((NXC * NYC - 1, SLOTS, 16, chan), BF16),
         pltpu.VMEM((NZR, SLOTS, 16, chan), BF16),

time: 38.1 us -> 38.3 us (level)
  no operation moved by 1% of the time
where the time goes in v7:
time: 38.3 us; the launch traced here: 38.2 us
  Pallas kernels  37.6 us (98%)
  between operations  0.64 us (2%)
    pallas_call x1, Pallas kernels, on_device(): pl.pallas_call(kernel, out_shape=tuple((pltpu.VMEM(one.shape, one.dtype)...  36.8 us
    pallas_call x1, Pallas kernels, on_device(): pl.pallas_call(write_out, out_shape=shapes, in_specs=[vmem, vmem], out_sp...  0.81 us

profile of v7, /device:TPU:1, one launch (start us, length us, event | category | flops | bytes accessed | tf_op | source)
XLA Modules:
  0.0 38.2 jit_solution(2205068765164264793)
XLA Ops:
  0.6 36.8 %shard_map.50 = (bf16[8,16,16,128]{3,2,1,0:T(8,128)(2,1)S(1)}, f32[27,4,128]{2,1,0:T(4,128)S(1)}) custom-call(f32[27,4,128]{2,1,0:T(4,128)} %bitcast.2, bf16[8,16,16,128]{3,2,1,0:T(8,128)(2,1)} %in_hbm.1, bf16[8,16,16,128]{3,2,1,0:T(8,128)(2,1)} %cot_hbm.1), custom_call_target="tpu_custom_call" | custom-call | tf_op jit(solution)/shard_map/pallas_call | solution.py:668
  37.4 0.8 %shard_map.51 = (bf16[8,16,16,128]{3,2,1,0:T(8,128)(2,1)}, f32[27,4,128]{2,1,0:T(4,128)}) custom-call(bf16[8,16,16,128]{3,2,1,0:T(8,128)(2,1)S(1)} %get-tuple-element.6.dx_ref, f32[27,4,128]{2,1,0:T(4,128)S(1)} %get-tuple-element.7.wg_ref), custom_call_target="tpu_custom_call" | custom-call | tf_op jit(solution)/shard_map/pallas_call | solution.py:681
